TPU v7x, 32 devices: a whole 2x2x4 slice. The times are simulated.
32 devices in a mesh: dp: 4 (over z), vocab: 8 (over y, x, core).
Axes of the slice: x: 2, y: 2, z: 4, core: 2. Of those that a mesh axis runs over, the one named last changes fastest.
Arguments:
- hidden: bfloat16 [3072, 896], P(('dp', 'vocab')), may hold values from -400 to 400
- target_ids: int32 [3072], P('dp'), may hold values from 0 to 151935
- owner: int32 [4, 24], P('dp'), may hold values from 0 to 23, each once within a row
- head: bfloat16 [896, 151936], P(None, 'vocab'), may hold values from -0.1875 to 0.1875
Outputs:
- owned_loss: float32 [96, 32], P(('dp', 'vocab'))
Inputs may be any that keep to these rules, and one draw needn't show every extreme that they name: Each row of owner names every slot once.
All inputs are finite; a program needn't handle non-finite values.
Results may differ from a plain program's by a relative error of at most 0.0003.
Values may be sent and summed in bfloat16 or wider, within the bound.
No kernel may reach another device: no remote copies, remote signals or barrier semaphores. Data moves between devices by JAX's collectives and lax.ppermute only.
A program may use at most 128 MiB of HBM per device.

v0:
```python
import math

import jax
import jax.numpy as jnp
from jax import lax
from jax.sharding import PartitionSpec as P


def local(hidden, target_ids, owner, head):
    width = head.shape[1]
    base = lax.axis_index("vocab") * width

    def partials(rows, labels):
        logits = jnp.dot(rows, head, preferred_element_type=jnp.float32)
        peak = jnp.max(logits, axis=1)
        expsum = jnp.sum(jnp.exp(logits - peak[:, None]), axis=1)
        column = lax.broadcasted_iota(jnp.int32, logits.shape, 1)
        picked = jnp.sum(jnp.where(column == (labels - base)[:, None], logits, 0.0), axis=1)
        return jnp.stack((peak, expsum, picked), 0)

    gathered = lax.all_gather(hidden, "vocab", axis=0, tiled=True)
    count = gathered.shape[0]
    step_rows = math.gcd(count, 512)
    split_rows = gathered.reshape(count // step_rows, step_rows, gathered.shape[1])
    split_labels = target_ids.reshape(count // step_rows, step_rows)
    results = lax.map(lambda pair: partials(pair[0], pair[1]), (split_rows, split_labels))
    stats = jnp.transpose(results, (1, 0, 2)).reshape(3, count)
    peak, expsum, picked = (stats[0], stats[1], stats[2])
    seq_group = owner.shape[1]
    length = target_ids.shape[0] // seq_group
    shards = lax.axis_size("vocab")
    own_count = seq_group // shards
    slots_row = owner[0]
    slot_index = lax.broadcasted_iota(jnp.int32, (seq_group, seq_group), 0)
    reorder = (slot_index == slots_row[None, :]).astype(jnp.float32)
    ordered_peak = jnp.dot(
        reorder, peak.reshape(seq_group, length), precision=lax.Precision.HIGHEST
    )
    ordered_sum = jnp.dot(
        reorder, expsum.reshape(seq_group, length), precision=lax.Precision.HIGHEST
    )
    ordered_pick = jnp.dot(
        reorder, picked.reshape(seq_group, length), precision=lax.Precision.HIGHEST
    )
    got_peak, got_sum, got_pick = (
        lax.all_to_all(ordered_peak, "vocab", split_axis=0, concat_axis=0, tiled=True),
        lax.all_to_all(ordered_sum, "vocab", split_axis=0, concat_axis=0, tiled=True),
        lax.all_to_all(ordered_pick, "vocab", split_axis=0, concat_axis=0, tiled=True),
    )
    got_peak = got_peak.reshape(shards, own_count, length)
    got_sum = got_sum.reshape(shards, own_count, length)
    got_pick = got_pick.reshape(shards, own_count, length)
    top = jnp.max(got_peak, axis=0)
    total = jnp.sum(got_sum * jnp.exp(got_peak - top[None]), axis=0)
    return top + jnp.log(total) - jnp.sum(got_pick, axis=0)


def solution(mesh):
    return jax.shard_map(
        local,
        mesh=mesh,
        in_specs=(P(("dp", "vocab"), None), P("dp"), P("dp", None), P(None, "vocab")),
        out_specs=P(("dp", "vocab"), None),
        check_vma=False,
    )
```

profile of v0, /device:TPU:0, one launch (start us, length us, event | category | flops | bytes accessed | tf_op | source)
XLA Modules:
  0.0 167.0 jit_solution(15133442570681837589)
XLA Ops:
  6.5 0.0 all-gather.2.cloned.1.call-start
  6.5 0.7 all-gather.2.cloned.1.call-update
  7.3 0.7 reshape.75
  8.0 28.7 %all-gather.2.cloned.1.call-done = bf16[768,896]{1,0:T(8,128)(2,1)} async-done(((bf16[96,896]{1,0:T(8,128)(2,1)}), bf16[768,896]{1,0:T(8,128)(2,1)}) %all-gather.2.cloned.1.call-update) | async-done | bytes 1376272 | tf_op jit(solution)/shard_map/all_gather | solution.py:21
  36.7 0.0 copy-start
  36.7 97.9 %while.10 = (s32[]{:T(128)}, f32[3,3,256]{2,1,0:T(4,128)S(1)}, bf16[3,256,896]{2,1,0:T(8,128)(2,1)}, bf16[896,18992]{0,1:T(8,128)(2,1)}, s32[3,256]{1,0:T(4,128)S(1)}, /*index=5*/s32[]{:T(128)}, s32[]{:T(128)}) while((s32[]{:T(128)}, f32[3,3,256]{2,1,0:T(4,128)S(1)}, bf16[3,256,896]{2,1,0:T(8,128)(2,1)}, bf16[896,18992]{0,1:T(8,128)(2,1)}, ...), condition=%wide.region_4.5_spmd, body=%wide.region_0.4_spmd.sunk | while | flops 8741791744 | bytes 73402960 | solution.py:26
  36.7 23.1 %fusion.26 = (f32[256]{0:T(256)S(1)}, f32[256,18992]{0,1:T(8,128)}) fusion(bf16[896,18992]{0,1:T(8,128)(2,1)} %get-tuple-element.119, bf16[3,256,896]{2,1,0:T(8,128)(2,1)} %get-tuple-element.118, s32[]{:T(128)} %get-tuple-element.109), kind=kOutput, calls=%fused_computation.28.clone.1 | convolution fusion | flops 8717479936 | bytes 53941760 | tf_op jit(solution)/shard_map/while/body/eval_jaxpr/dot_general | solution.py:14
  59.8 9.5 %exponential_reduce_fusion.2 = (f32[256]{0:T(256)S(1)}, f32[256]{0:T(256)S(1)}) fusion(f32[256,18992]{0,1:T(8,128)} %get-tuple-element.98, f32[256]{0:T(256)S(1)} %get-tuple-element.99, s32[256]{0:T(256)S(1)} %bitcast.37), kind=kLoop, calls=%fused_computation.2.clone.1 | loop fusion | flops 24309248 | bytes 19451904 | tf_op jit(solution)/shard_map/while/body/eval_jaxpr/reduce_sum | solution.py:16
  69.4 23.1 %fusion.26 = (f32[256]{0:T(256)S(1)}, f32[256,18992]{0,1:T(8,128)}) fusion(bf16[896,18992]{0,1:T(8,128)(2,1)} %get-tuple-element.119, bf16[3,256,896]{2,1,0:T(8,128)(2,1)} %get-tuple-element.118, s32[]{:T(128)} %get-tuple-element.109), kind=kOutput, calls=%fused_computation.28.clone.1 | convolution fusion | flops 8717479936 | bytes 53941760 | tf_op jit(solution)/shard_map/while/body/eval_jaxpr/dot_general | solution.py:14
  92.4 9.5 %exponential_reduce_fusion.2 = (f32[256]{0:T(256)S(1)}, f32[256]{0:T(256)S(1)}) fusion(f32[256,18992]{0,1:T(8,128)} %get-tuple-element.98, f32[256]{0:T(256)S(1)} %get-tuple-element.99, s32[256]{0:T(256)S(1)} %bitcast.37), kind=kLoop, calls=%fused_computation.2.clone.1 | loop fusion | flops 24309248 | bytes 19451904 | tf_op jit(solution)/shard_map/while/body/eval_jaxpr/reduce_sum | solution.py:16
  102.0 23.0 %fusion.26 = (f32[256]{0:T(256)S(1)}, f32[256,18992]{0,1:T(8,128)}) fusion(bf16[896,18992]{0,1:T(8,128)(2,1)} %get-tuple-element.119, bf16[3,256,896]{2,1,0:T(8,128)(2,1)} %get-tuple-element.118, s32[]{:T(128)} %get-tuple-element.109), kind=kOutput, calls=%fused_computation.28.clone.1 | convolution fusion | flops 8717479936 | bytes 53941760 | tf_op jit(solution)/shard_map/while/body/eval_jaxpr/dot_general | solution.py:14
  125.0 9.5 %exponential_reduce_fusion.2 = (f32[256]{0:T(256)S(1)}, f32[256]{0:T(256)S(1)}) fusion(f32[256,18992]{0,1:T(8,128)} %get-tuple-element.98, f32[256]{0:T(256)S(1)} %get-tuple-element.99, s32[256]{0:T(256)S(1)} %bitcast.37), kind=kLoop, calls=%fused_computation.2.clone.1 | loop fusion | flops 24309248 | bytes 19451904 | tf_op jit(solution)/shard_map/while/body/eval_jaxpr/reduce_sum | solution.py:16
  134.6 0.1 reshape.76
  134.7 0.0 copy-done
  134.7 0.2 fusion.9
  134.9 0.6 copy.5
  135.5 3.3 %all-to-all-start = ((f32[8,3,32]{2,1,0:T(4,128)}), f32[8,3,32]{2,1,0:T(4,128)S(1)}, u32[]{:S(2)}, u32[]{:S(2)}) async-start(f32[8,3,32]{2,1,0:T(4,128)} %copy.5), calls=%async_computation | async-start | bytes 32768 | tf_op jit(solution)/shard_map/all_to_all | solution.py:46
  138.9 0.1 reshape.77
  138.9 0.2 fusion.7
  139.1 0.6 copy.6
  139.7 0.1 reshape.78
  139.8 3.7 %all-to-all-done = f32[8,3,32]{2,1,0:T(4,128)S(1)} async-done(((f32[8,3,32]{2,1,0:T(4,128)}), f32[8,3,32]{2,1,0:T(4,128)S(1)}, u32[]{:S(2)}, u32[]{:S(2)}) %all-to-all-start) | async-done | bytes 3104 | tf_op jit(solution)/shard_map/all_to_all | solution.py:46
  143.5 3.3 %all-to-all-start.1 = ((f32[8,3,32]{2,1,0:T(4,128)}), f32[8,3,32]{2,1,0:T(4,128)S(1)}, u32[]{:S(2)}, u32[]{:S(2)}) async-start(f32[8,3,32]{2,1,0:T(4,128)} %copy.6), calls=%async_computation.1 | async-start | bytes 32768 | tf_op jit(solution)/shard_map/all_to_all | solution.py:47
  146.9 0.2 fusion.5
  147.1 0.6 copy.7
  147.7 3.9 %all-to-all-done.1 = f32[8,3,32]{2,1,0:T(4,128)S(1)} async-done(((f32[8,3,32]{2,1,0:T(4,128)}), f32[8,3,32]{2,1,0:T(4,128)S(1)}, u32[]{:S(2)}, u32[]{:S(2)}) %all-to-all-start.1) | async-done | bytes 3104 | tf_op jit(solution)/shard_map/all_to_all | solution.py:47
  151.6 3.3 %all-to-all-start.2 = ((f32[8,3,32]{2,1,0:T(4,128)}), f32[8,3,32]{2,1,0:T(4,128)S(1)}, u32[]{:S(2)}, u32[]{:S(2)}) async-start(f32[8,3,32]{2,1,0:T(4,128)} %copy.7), calls=%async_computation.2 | async-start | bytes 32768 | tf_op jit(solution)/shard_map/all_to_all | solution.py:48
  154.9 4.7 %all-to-all-done.2 = f32[8,3,32]{2,1,0:T(4,128)S(1)} async-done(((f32[8,3,32]{2,1,0:T(4,128)}), f32[8,3,32]{2,1,0:T(4,128)S(1)}, u32[]{:S(2)}, u32[]{:S(2)}) %all-to-all-start.2) | async-done | bytes 3104 | tf_op jit(solution)/shard_map/all_to_all | solution.py:48
  159.6 0.6 add_subtract_fusion
  (12 shorter events, 0.2 us)
Async XLA Ops:
  6.5 30.2 %all-gather.2.cloned.1.call-start = ((), (), s32[]{:S(2)}) async-start(), calls=%async_computation.3 | async-start | bytes 1548288 | tf_op jit(solution)/shard_map/all_gather | solution.py:21
  36.7 98.0 %copy-start = (s32[1,24]{1,0:T(1,128)S(1)}, s32[1,24]{1,0:T(1,128)}, u32[]{:S(2)}) copy-start(s32[1,24]{1,0:T(1,128)} %param.8) | copy-start | bytes 292
  135.5 8.0 %all-to-all-start = ((f32[8,3,32]{2,1,0:T(4,128)}), f32[8,3,32]{2,1,0:T(4,128)S(1)}, u32[]{:S(2)}, u32[]{:S(2)}) async-start(f32[8,3,32]{2,1,0:T(4,128)} %copy.5), calls=%async_computation | async-start | bytes 32768 | tf_op jit(solution)/shard_map/all_to_all | solution.py:46
  143.5 8.0 %all-to-all-start.1 = ((f32[8,3,32]{2,1,0:T(4,128)}), f32[8,3,32]{2,1,0:T(4,128)S(1)}, u32[]{:S(2)}, u32[]{:S(2)}) async-start(f32[8,3,32]{2,1,0:T(4,128)} %copy.6), calls=%async_computation.1 | async-start | bytes 32768 | tf_op jit(solution)/shard_map/all_to_all | solution.py:47
  151.6 8.0 %all-to-all-start.2 = ((f32[8,3,32]{2,1,0:T(4,128)}), f32[8,3,32]{2,1,0:T(4,128)S(1)}, u32[]{:S(2)}, u32[]{:S(2)}) async-start(f32[8,3,32]{2,1,0:T(4,128)} %copy.7), calls=%async_computation.2 | async-start | bytes 32768 | tf_op jit(solution)/shard_map/all_to_all | solution.py:48
Sparse Core Ops, SparseCore 0:
  9.2 27.4 all-gather.1
where the time goes:
time: 168 us; the launch traced here: 167 us
  matrix products  69.7 us (41%)
  waiting for transfers between devices  41.7 us (25%)
  other arithmetic  29.3 us (17%)
  between operations  13.5 us (8%)
  starting transfers between devices  9.98 us (6%)
  local copies, waits for them, and re-layouts  2.83 us (2%)
    dot_general x3, matrix products, partials(): logits = jnp.dot(rows, head, preferred_element_type=jnp.float32)  69.2 us
    all_gather x1, waiting for transfers between devices, local(): gathered = lax.all_gather(hidden, 'vocab', axis=0, tiled=True)  28.7 us
    reduce_sum x3, other arithmetic, partials(): expsum = jnp.sum(jnp.exp(logits - peak[:, None]), axis=1)  28.5 us
    all_to_all x1, waiting for transfers between devices, local(): lax.all_to_all(ordered_pick, 'vocab', split_axis=0, concat_axis=0, tiled=...  4.66 us
    all_to_all x1, waiting for transfers between devices, local(): lax.all_to_all(ordered_sum, 'vocab', split_axis=0, concat_axis=0, tiled=T...  3.86 us
    all_to_all x1, waiting for transfers between devices, local(): lax.all_to_all(ordered_peak, 'vocab', split_axis=0, concat_axis=0, tiled=...  3.72 us
  transfers between devices with their start and end apart: 4, of which 4 were waited for; matrix products, arithmetic and copies ran while one was open for 1% of the time, Pallas kernels for 0%

commit v1 on v0

v1 whole, which is shorter than its diff:
```python
import functools
import math

import jax
import jax.numpy as jnp
from jax import lax
from jax.experimental import pallas as pl
from jax.experimental.pallas import tpu as pltpu
from jax.sharding import PartitionSpec as P

LOG2E = math.log2(math.e)
FLOOR = -1e30


def tree(op, values):
    while len(values) > 1:
        paired = [op(a, b) for a, b in zip(values[::2], values[1::2])]
        values = paired + ([values[-1]] if len(values) % 2 else [])
    return values[0]


def head_kernel(x_ref, lab_ref, w_ref, o_ref, m_ref, s_ref, p_ref, lb_ref, xt_ref, *, chunk, width, group):
    tokens = x_ref.shape[0]
    block = w_ref.shape[0]
    step, steps = pl.program_id(0), pl.num_programs(0)

    @pl.when(step == 0)
    def _():
        labels = lab_ref[...]
        labels = jnp.where((labels >= 0) & (labels < width), labels, -(1 << 30))
        lb_ref[...] = jnp.broadcast_to(labels, lb_ref.shape)
        m_ref[...] = jnp.full_like(m_ref, FLOOR)
        s_ref[...] = jnp.zeros_like(s_ref)
        p_ref[...] = jnp.zeros_like(p_ref)
        xt_ref[...] = x_ref[...].T

    sub = lax.broadcasted_iota(jnp.int32, (8, 128), 0)

    def run(masked):
        for r0 in range(0, block, chunk):
            logits = jnp.dot(w_ref[r0 : r0 + chunk, :], xt_ref[...], preferred_element_type=jnp.float32)
            for c in range(tokens // 128):
                cols = slice(c * 128, (c + 1) * 128)
                label, pick, top, total = lb_ref[:, cols], p_ref[:, cols], m_ref[:, cols], s_ref[:, cols]
                for g in range(0, chunk, group):
                    scaled = []
                    for r in range(g, min(g + group, chunk), 8):
                        value = logits[r : r + 8, cols]
                        row = sub + (step * block + r0 + r)
                        pick = jnp.where(label == row, value, pick)
                        value = value * LOG2E
                        if masked:
                            value = jnp.where(row < width, value, FLOOR)
                        scaled.append(value)
                    peak = jnp.maximum(top, tree(jnp.maximum, scaled))
                    total = total * jnp.exp2(top - peak) + tree(jnp.add, [jnp.exp2(v - peak) for v in scaled])
                    top = peak
                p_ref[:, cols], m_ref[:, cols], s_ref[:, cols] = pick, top, total

    @pl.when(step < steps - 1)
    def _():
        run(False)

    @pl.when(step == steps - 1)
    def _():
        run(width % block != 0)
        top = m_ref[...]
        peak = jnp.max(top, axis=0, keepdims=True)
        total = jnp.sum(s_ref[...] * jnp.exp2(top - peak), axis=0, keepdims=True)
        o_ref[0:1, :] = (peak + jnp.log2(total)) * (1.0 / LOG2E)
        o_ref[1:2, :] = jnp.sum(p_ref[...], axis=0, keepdims=True)


def head_stats(x, labels, rows):
    tokens, depth = x.shape
    width = rows.shape[0]
    block, chunk = 1920, 192
    return pl.pallas_call(
        functools.partial(head_kernel, chunk=chunk, width=width, group=48),
        out_shape=jax.ShapeDtypeStruct((2, tokens), jnp.float32),
        grid=(pl.cdiv(width, block),),
        in_specs=[
            pl.BlockSpec((tokens, depth), lambda j: (0, 0)),
            pl.BlockSpec((1, tokens), lambda j: (0, 0)),
            pl.BlockSpec((block, depth), lambda j: (j, 0)),
        ],
        out_specs=pl.BlockSpec((2, tokens), lambda j: (0, 0)),
        scratch_shapes=[pltpu.VMEM((8, tokens), jnp.float32)] * 3
        + [pltpu.VMEM((8, tokens), jnp.int32), pltpu.VMEM((depth, tokens), x.dtype)],
        compiler_params=pltpu.CompilerParams(vmem_limit_bytes=60 << 20),
    )(x, labels, rows)


def local(hidden, target_ids, owner, head):
    shards, me = lax.axis_size("vocab"), lax.axis_index("vocab")
    width = head.shape[1]
    count = hidden.shape[0]
    seq_group = owner.shape[1]
    own_count = seq_group // shards
    length = target_ids.shape[0] // seq_group

    def swap(v, k):
        return lax.ppermute(v, "vocab", [(i, i ^ k) for i in range(shards)])

    places = list(range(0, shards, 2)) + list(range(1, shards, 2))
    even = [hidden] + [swap(hidden, k) for k in range(2, shards, 2)]
    x = jnp.concatenate(even + [swap(v, 1) for v in even], 0)
    labels = jnp.concatenate([lax.dynamic_slice_in_dim(target_ids, (me ^ k) * count, count) for k in places])
    stats = head_stats(x, (labels - me * width)[None, :], head.T)

    per_shard = count // length
    slots = jnp.concatenate([lax.dynamic_slice_in_dim(owner[0], (me ^ k) * per_shard, per_shard) for k in places])
    onehot = (lax.broadcasted_iota(jnp.int32, (seq_group, seq_group), 0) == slots[None, :]).astype(jnp.float32)
    by_seq = stats.reshape(2, seq_group, length).transpose(1, 0, 2).reshape(seq_group, 2 * length)
    send = jnp.dot(onehot, by_seq, precision=lax.Precision.HIGHEST)
    got = lax.all_to_all(send, "vocab", split_axis=0, concat_axis=0, tiled=True)
    got = got.reshape(shards, own_count, 2, length)
    parts, picked = got[:, :, 0], got[:, :, 1]
    top = jnp.max(parts, axis=0)
    return top + jnp.log(jnp.sum(jnp.exp(parts - top[None]), axis=0)) - jnp.sum(picked, axis=0)


def solution(mesh):
    return jax.shard_map(
        local,
        mesh=mesh,
        in_specs=(P(("dp", "vocab"), None), P("dp"), P("dp", None), P(None, "vocab")),
        out_specs=P(("dp", "vocab"), None),
        check_vma=False,
    )
```

time: 168 us -> 66.2 us (0.39)
  matrix products: 69.7 us -> 0.18 us
  Pallas kernels: 0 us -> 40 us
  waiting for transfers between devices: 41.7 us -> 4.65 us
  other arithmetic: 29.3 us -> 1.92 us
  between operations: 13.5 us -> 0.18 us
  blocking collectives: 0 us -> 7.3 us
  starting transfers between devices: 9.98 us -> 5.58 us
  local copies, waits for them, and re-layouts: 2.83 us -> 6.16 us
    dot_general x6 -> x1, matrix products: 69.7 us -> 0.18 us  [local(): send = jnp.dot(onehot, by_seq, precision=lax.Precision.HIGHEST)]
    pallas_call x0 -> x1, Pallas kernels: none -> 40 us  [head_stats(): pl.pallas_call(functools.partial(head_kernel, chunk=chunk, width=width, g...]
    all_gather x1 -> x0, waiting for transfers between devices: 28.7 us -> none  [local(): gathered = lax.all_gather(hidden, 'vocab', axis=0, tiled=True)]
    reduce_sum x5 -> x1, other arithmetic: 28.6 us -> 0.02 us  [local(): jnp.sum(jnp.exp(parts - top[None]), axis=0)]
    all_to_all x3 -> x0, waiting for transfers between devices: 12.2 us -> none  [the longest x1 4.66 us: local(): lax.all_to_all(ordered_pick, 'vocab', split_axis=0, concat_axis=0, tiled=...]
    all_to_all x3 -> x0, starting transfers between devices: 9.98 us -> none  [the longest x1 3.33 us: local(): lax.all_to_all(ordered_sum, 'vocab', split_axis=0, concat_axis=0, tiled=T...]
    all_to_all x0 -> x1, blocking collectives: none -> 7.3 us  [local(): got = lax.all_to_all(send, 'vocab', split_axis=0, concat_axis=0, tiled=True)]
    ppermute x0 -> x7, starting transfers between devices: none -> 5.58 us  [swap(): return lax.ppermute(v, 'vocab', [(i, i ^ k) for i in range(shards)])]
  transfers between devices with their start and end apart: 4 -> 7, of which waited for: 4 -> 3; matrix products, arithmetic and copies ran while one was open for 1% -> 6% of each run, Pallas kernels for 0% -> 0%
where the time goes in v1:
time: 66.2 us; the launch traced here: 66 us
  Pallas kernels  40 us (60%)
  blocking collectives  7.3 us (11%)
  local copies, waits for them, and re-layouts  6.16 us (9%)
  starting transfers between devices  5.58 us (8%)
  waiting for transfers between devices  4.65 us (7%)
  other arithmetic  1.92 us (3%)
    pallas_call x1, Pallas kernels, head_stats(): pl.pallas_call(functools.partial(head_kernel, chunk=chunk, width=width, g...  40 us
    all_to_all x1, blocking collectives, local(): got = lax.all_to_all(send, 'vocab', split_axis=0, concat_axis=0, tiled=True)  7.3 us
    ppermute x7, starting transfers between devices, swap(): return lax.ppermute(v, 'vocab', [(i, i ^ k) for i in range(shards)])  5.58 us
    ppermute x7, waiting for transfers between devices, swap(): return lax.ppermute(v, 'vocab', [(i, i ^ k) for i in range(shards)])  4.65 us
    unnamed x11, local copies, waits for them, and re-layouts  2.37 us
  transfers between devices with their start and end apart: 7, of which 3 were waited for; matrix products, arithmetic and copies ran while one was open for 6% of the time, Pallas kernels for 0%

profile of v1, /device:TPU:0, one launch (start us, length us, event | category | flops | bytes accessed | tf_op | source)
XLA Modules:
  0.0 66.0 jit_solution(9154161908200095362)
XLA Ops:
  0.0 3.0 %collective-permute-start = (bf16[96,896]{1,0:T(8,128)(2,1)}, bf16[96,896]{1,0:T(8,128)(2,1)S(1)}, u32[]{:S(2)}, u32[]{:S(2)}) collective-permute-start(bf16[96,896]{1,0:T(8,128)(2,1)} %param.4), channel_id=1, source_target_pairs={{0,2},{1,3},{2,0},{3,1},{4,6},{5,7},{6,4},{7,5},{8,10},{9,11},{10,... | collective-permute-start | bytes 516104 | tf_op jit(solution)/shard_map/ppermute | solution.py:103
  3.0 1.5 %collective-permute-start.1 = (bf16[96,896]{1,0:T(8,128)(2,1)}, bf16[96,896]{1,0:T(8,128)(2,1)S(1)}, u32[]{:S(2)}, u32[]{:S(2)}) collective-permute-start(bf16[96,896]{1,0:T(8,128)(2,1)} %param.4), channel_id=1, source_target_pairs={{0,4},{1,5},{2,6},{3,7},{4,0},{5,1},{6,2},{7,3},{8,12},{9,13},{10,... | collective-permute-start | bytes 516104 | tf_op jit(solution)/shard_map/ppermute | solution.py:103
  4.5 0.0 collective-permute-start.2
  4.5 0.0 collective-permute-start.3
  4.5 1.0 %constant_dynamic-update-slice_fusion.7 = bf16[768,896]{1,0:T(8,128)(2,1)S(1)} fusion(bf16[96,896]{1,0:T(8,128)(2,1)} %param.4), kind=kLoop, calls=%fused_computation.7 | loop fusion | bytes 344064
  5.6 1.1 %dynamic-slice_bitcast_fusion = (s32[1,96]{1,0:T(1,128)S(1)}, s32[1,96]{1,0:T(1,128)S(1)}, s32[1,96]{1,0:T(1,128)S(1)}, s32[1,96]{1,0:T(1,128)S(1)}, s32[1,96]{1...) fusion(s32[768]{0:T(1024)} %param.5, s32[]{:T(128)S(6)} %select_n.63, ...), kind=kLoop, calls=%fused_computation.33 | loop fusion | bytes 6176 | tf_op jit(solution)/shard_map/concatenate | solution.py:108
  6.6 0.1 concatenate.42
  6.8 0.6 broadcast_subtract_fusion.lab_ref
  7.3 1.0 %fusion.11 = (s32[3]{0:T(128)S(1)}, s32[3]{0:T(128)S(1)}, s32[3]{0:T(128)S(1)}, s32[3]{0:T(128)S(1)}, s32[3]{0:T(128)S(1)}, /*index=5*/s32[3]{0:T(128)S(1)}, s32[3]{0:T(128)S(1)}, s32[3]{0:T(128)S(1)}) fusion(s32[1,24]{1,0:T(1,128)} %param.6, s32[]{:T(128)S(6)} %select_n.55, s32[]{:T(128)S(6)} %select_n.53, s32[]{:T(128)S(6)} %select_n.52, s32[]{:T(128)S(6)} %select_n.51, ...), kind=kLoop, calls=%fused_computation.32 | loop fusion | bytes 224 | tf_op jit(solution)/shard_map/dynamic_slice | solution.py:112
  8.4 0.1 concatenate.32
  8.4 0.0 collective-permute-done
  8.4 0.5 collective-permute-start.4
  9.0 3.7 %collective-permute-done.1 = bf16[96,896]{1,0:T(8,128)(2,1)S(1)} collective-permute-done((bf16[96,896]{1,0:T(8,128)(2,1)}, bf16[96,896]{1,0:T(8,128)(2,1)S(1)}, u32[]{:S(2)}, u32[]{:S(2)}) %collective-permute-start.1) | collective-permute-done | bytes 172064 | tf_op jit(solution)/shard_map/ppermute | solution.py:103
  12.7 0.0 collective-permute-start.5
  12.7 0.0 collective-permute-done.2
  12.7 0.6 collective-permute-start.6
  13.3 0.0 collective-permute-done.3
  13.4 0.0 collective-permute-done.4
  13.4 0.7 %collective-permute-done.5 = bf16[96,896]{1,0:T(8,128)(2,1)S(1)} collective-permute-done((bf16[96,896]{1,0:T(8,128)(2,1)S(1)}, bf16[96,896]{1,0:T(8,128)(2,1)S(1)}, u32[]{:S(2)}, u32[]{:S(2)}) %collective-permute-start.5) | collective-permute-done | bytes 172064 | tf_op jit(solution)/shard_map/ppermute | solution.py:103
  14.1 0.2 collective-permute-done.6
  14.4 1.1 %copy-done = bf16[768,896]{1,0:T(8,128)(2,1)} copy-done((bf16[768,896]{1,0:T(8,128)(2,1)}, bf16[768,896]{1,0:T(8,128)(2,1)S(1)}, u32[]{:S(2)}) %copy-start) | copy-done | bytes 1376280
  15.5 40.0 %shard_map.46 = f32[2,768]{1,0:T(2,128)} custom-call(bf16[768,896]{1,0:T(8,128)(2,1)} %copy-done, s32[1,768]{1,0:T(1,128)} %broadcast_subtract_fusion.lab_ref, bf16[18992,896]{1,0:T(8,128)(2,1)} %bitcast.38), custom_call_target="tpu_custom_call" | custom-call | tf_op jit(solution)/shard_map/pallas_call | solution.py:78
  55.5 0.8 %reshape.147 = f32[2,24,32]{2,1,0:T(8,128)S(1)} reshape(f32[2,768]{1,0:T(2,128)} %shard_map.46) | data formatting | bytes 12288 | tf_op jit(solution)/shard_map/reshape | solution.py:114
  56.2 0.1 reshape.150
  56.3 0.2 fusion
  56.5 0.1 reshape.152
  56.6 7.3 %all_to_all.6 = f32[8,1,192]{2,1,0:T(1,128)S(1)} all-to-all(f32[8,1,192]{2,1,0:T(1,128)S(1)} %reshape.152), channel_id=1, replica_groups=mesh['dp'=4,'vocab'=8] {'vocab'}, dimensions={0} | all-to-all | bytes 12288 | tf_op jit(solution)/shard_map/all_to_all | solution.py:116
  63.9 0.5 broadcast.28
  64.4 0.7 %reduce.2 = f32[8,192]{1,0:T(8,128)S(1)} reduce(f32[8,1,192]{2,1,0:T(1,128)S(1)} %all_to_all.6, f32[]{:T(128)} %broadcast.28), dimensions={1}, to_apply=%all_to_all.4.reduce_sub_computation | reduce | bytes 12292 | tf_op jit(solution)/shard_map/all_to_all | solution.py:116
  65.1 0.1 reshape.153
  65.2 0.1 reshape.149
  65.4 0.6 add_subtract_fusion
  (14 shorter events, 0.3 us)
Async XLA Ops:
  0.0 8.4 %collective-permute-start = (bf16[96,896]{1,0:T(8,128)(2,1)}, bf16[96,896]{1,0:T(8,128)(2,1)S(1)}, u32[]{:S(2)}, u32[]{:S(2)}) collective-permute-start(bf16[96,896]{1,0:T(8,128)(2,1)} %param.4), channel_id=1, source_target_pairs={{0,2},{1,3},{2,0},{3,1},{4,6},{5,7},{6,4},{7,5},{8,10},{9,11},{10,... | collective-permute-start | bytes 516104 | tf_op jit(solution)/shard_map/ppermute | solution.py:103
  3.0 9.7 %collective-permute-start.1 = (bf16[96,896]{1,0:T(8,128)(2,1)}, bf16[96,896]{1,0:T(8,128)(2,1)S(1)}, u32[]{:S(2)}, u32[]{:S(2)}) collective-permute-start(bf16[96,896]{1,0:T(8,128)(2,1)} %param.4), channel_id=1, source_target_pairs={{0,4},{1,5},{2,6},{3,7},{4,0},{5,1},{6,2},{7,3},{8,12},{9,13},{10,... | collective-permute-start | bytes 516104 | tf_op jit(solution)/shard_map/ppermute | solution.py:103
  4.5 8.2 %collective-permute-start.2 = (bf16[96,896]{1,0:T(8,128)(2,1)}, bf16[96,896]{1,0:T(8,128)(2,1)S(1)}, u32[]{:S(2)}, u32[]{:S(2)}) collective-permute-start(bf16[96,896]{1,0:T(8,128)(2,1)} %param.4), channel_id=1, source_target_pairs={{0,6},{1,7},{2,4},{3,5},{4,2},{5,3},{6,0},{7,1},{8,14},{9,15},{10,... | collective-permute-start | bytes 516104 | tf_op jit(solution)/shard_map/ppermute | solution.py:103
  4.5 8.8 %collective-permute-start.3 = (bf16[96,896]{1,0:T(8,128)(2,1)}, bf16[96,896]{1,0:T(8,128)(2,1)S(1)}, u32[]{:S(2)}, u32[]{:S(2)}) collective-permute-start(bf16[96,896]{1,0:T(8,128)(2,1)} %param.4), channel_id=1, source_target_pairs={{0,1},{1,0},{2,3},{3,2},{4,5},{5,4},{6,7},{7,6},{8,9},{9,8},{10,11... | collective-permute-start | bytes 516104 | tf_op jit(solution)/shard_map/ppermute | solution.py:103
  8.4 4.9 %collective-permute-start.4 = (bf16[96,896]{1,0:T(8,128)(2,1)S(1)}, bf16[96,896]{1,0:T(8,128)(2,1)S(1)}, u32[]{:S(2)}, u32[]{:S(2)}) collective-permute-start(bf16[96,896]{1,0:T(8,128)(2,1)S(1)} %collective-permute-done), channel_id=1, source_target_pairs={{0,1},{1,0},{2,3},{3,2},{4,5},{5,4},{6,7},{7,6},{8,9},{9,8},{10,11... | collective-permute-start | bytes 516104 | tf_op jit(solution)/shard_map/ppermute | solution.py:103
  12.7 1.4 %collective-permute-start.5 = (bf16[96,896]{1,0:T(8,128)(2,1)S(1)}, bf16[96,896]{1,0:T(8,128)(2,1)S(1)}, u32[]{:S(2)}, u32[]{:S(2)}) collective-permute-start(bf16[96,896]{1,0:T(8,128)(2,1)S(1)} %collective-permute-done.1), channel_id=1, source_target_pairs={{0,1},{1,0},{2,3},{3,2},{4,5},{5,4},{6,7},{7,6},{8,9},{9,8},{10,11... | collective-permute-start | bytes 516104 | tf_op jit(solution)/shard_map/ppermute | solution.py:103
  12.7 1.6 %collective-permute-start.6 = (bf16[96,896]{1,0:T(8,128)(2,1)S(1)}, bf16[96,896]{1,0:T(8,128)(2,1)S(1)}, u32[]{:S(2)}, u32[]{:S(2)}) collective-permute-start(bf16[96,896]{1,0:T(8,128)(2,1)S(1)} %collective-permute-done.2), channel_id=1, source_target_pairs={{0,1},{1,0},{2,3},{3,2},{4,5},{5,4},{6,7},{7,6},{8,9},{9,8},{10,11... | collective-permute-start | bytes 516104 | tf_op jit(solution)/shard_map/ppermute | solution.py:103
  14.4 1.1 %copy-start = (bf16[768,896]{1,0:T(8,128)(2,1)}, bf16[768,896]{1,0:T(8,128)(2,1)S(1)}, u32[]{:S(2)}) copy-start(bf16[768,896]{1,0:T(8,128)(2,1)S(1)} %constant_dynamic-update-slice_fusion.x_ref) | copy-start | bytes 4128772

commit v2 on v1

v2 whole, which is shorter than its diff:
```python
import functools
import math

import jax
import jax.numpy as jnp
from jax import lax
from jax.experimental import pallas as pl
from jax.experimental.pallas import tpu as pltpu
from jax.sharding import PartitionSpec as P

LOG2E = math.log2(math.e)
FLOOR = -1e30


def tree(op, values):
    while len(values) > 1:
        paired = [op(a, b) for a, b in zip(values[::2], values[1::2])]
        values = paired + ([values[-1]] if len(values) % 2 else [])
    return values[0]


def head_kernel(*refs, pieces, chunk, width, group, length):
    parts, (lab_ref, slot_ref, w_ref, o_ref, m_ref, s_ref, p_ref, lb_ref, x_ref, xt_ref) = refs[:pieces], refs[pieces:]
    tokens = x_ref.shape[0]
    block = w_ref.shape[0]
    step, steps = pl.program_id(0), pl.num_programs(0)

    def labels():
        value = lab_ref[...]
        return jnp.where((value >= 0) & (value < width), value, -(1 << 30))

    @pl.when(step == 0)
    def _():
        at = 0
        for part in parts:
            x_ref[at : at + part.shape[0], :] = part[...]
            at += part.shape[0]
        lb_ref[...] = jnp.broadcast_to(jnp.right_shift(labels(), 3), lb_ref.shape)
        m_ref[...] = jnp.full_like(m_ref, FLOOR)
        s_ref[...] = jnp.zeros_like(s_ref)
        p_ref[...] = jnp.zeros_like(p_ref)
        xt_ref[...] = x_ref[...].T

    sub = lax.broadcasted_iota(jnp.int32, (8, 128), 0)

    def run(masked):
        for r0 in range(0, block, chunk):
            logits = jnp.dot(w_ref[r0 : r0 + chunk, :], xt_ref[...], preferred_element_type=jnp.float32)
            for c in range(tokens // 128):
                cols = slice(c * 128, (c + 1) * 128)
                pick, top, total = p_ref[:, cols], m_ref[:, cols], s_ref[:, cols]
                label = lb_ref[:, cols] - (step * (block // 8) + r0 // 8)
                for g in range(0, chunk, group):
                    values = []
                    for r in range(g, min(g + group, chunk), 8):
                        value = logits[r : r + 8, cols]
                        if masked:
                            value = jnp.where(sub + (step * block + r0 + r) < width, value, FLOOR)
                        pick = jnp.where(label == r // 8, value, pick)
                        values.append(value)
                    peak = jnp.maximum(top, tree(jnp.maximum, values))
                    fresh = tree(jnp.add, [jnp.exp2((v - peak) * LOG2E) for v in values])
                    total = total * jnp.exp2((top - peak) * LOG2E) + fresh
                    top = peak
                p_ref[:, cols], m_ref[:, cols], s_ref[:, cols] = pick, top, total

    @pl.when(step < steps - 1)
    def _():
        run(False)

    @pl.when(step == steps - 1)
    def _():
        run(width % block != 0)
        top = m_ref[...]
        peak = jnp.max(top, axis=0, keepdims=True)
        total = jnp.sum(s_ref[...] * jnp.exp2((top - peak) * LOG2E), axis=0, keepdims=True)
        lse = peak + jnp.log(total)
        eight = lax.broadcasted_iota(jnp.int32, p_ref.shape, 0)
        picked = jnp.sum(jnp.where((labels() & 7) == eight, p_ref[...], 0.0), axis=0, keepdims=True)
        slots = o_ref.shape[0]
        mine = lax.broadcasted_iota(jnp.int32, (slots, tokens), 0) == slot_ref[...]
        token = lax.broadcasted_iota(jnp.int32, (tokens, length), 0)
        lane = lax.broadcasted_iota(jnp.int32, (tokens, length), 1)
        spread = (lax.rem(token, length) == lane).astype(jnp.float32)
        for k, row in enumerate((lse, picked)):
            o_ref[:, k * length : (k + 1) * length] = jnp.dot(
                jnp.where(mine, row, 0.0), spread, precision=lax.Precision.HIGHEST, preferred_element_type=jnp.float32
            )


def head_stats(parts, labels, slots, rows, slot_count, length):
    tokens, depth = labels.shape[1], rows.shape[1]
    width = rows.shape[0]
    block, chunk = 3168, 144
    return pl.pallas_call(
        functools.partial(head_kernel, pieces=len(parts), chunk=chunk, width=width, group=24, length=length),
        out_shape=jax.ShapeDtypeStruct((slot_count, 2 * length), jnp.float32),
        grid=(pl.cdiv(width, block),),
        in_specs=[pl.BlockSpec(part.shape, lambda j: (0, 0)) for part in parts]
        + [
            pl.BlockSpec((1, tokens), lambda j: (0, 0)),
            pl.BlockSpec((1, tokens), lambda j: (0, 0)),
            pl.BlockSpec((block, depth), lambda j: (j, 0)),
        ],
        out_specs=pl.BlockSpec((slot_count, 2 * length), lambda j: (0, 0)),
        scratch_shapes=[pltpu.VMEM((8, tokens), jnp.float32)] * 3
        + [
            pltpu.VMEM((8, tokens), jnp.int32),
            pltpu.VMEM((tokens, depth), parts[0].dtype),
            pltpu.VMEM((depth, tokens), parts[0].dtype),
        ],
        compiler_params=pltpu.CompilerParams(vmem_limit_bytes=60 << 20),
    )(*parts, labels, slots, rows)


def combine_kernel(got_ref, o_ref):
    length = o_ref.shape[1]
    parts, picked = got_ref[:, :, :length], got_ref[:, :, length:]
    top = jnp.max(parts, axis=0)
    o_ref[...] = top + jnp.log(jnp.sum(jnp.exp(parts - top[None]), axis=0)) - jnp.sum(picked, axis=0)


def local(hidden, target_ids, owner, head):
    shards, me = lax.axis_size("vocab"), lax.axis_index("vocab")
    width = head.shape[1]
    count = hidden.shape[0]
    seq_group = owner.shape[1]
    own_count = seq_group // shards
    length = target_ids.shape[0] // seq_group

    def swap(v, k):
        return lax.ppermute(v, "vocab", [(i, i ^ k) for i in range(shards)])

    places = list(range(0, shards, 2)) + list(range(1, shards, 2))
    even = [hidden] + [swap(hidden, k) for k in range(2, shards, 2)]
    parts = even + [swap(v, 1) for v in even]
    per_shard = count // length
    labels = jnp.concatenate([lax.dynamic_slice_in_dim(target_ids, (me ^ k) * count, count) for k in places])
    slots = jnp.concatenate([lax.dynamic_slice_in_dim(owner[0], (me ^ k) * per_shard, per_shard) for k in places])
    slots = jnp.broadcast_to(slots[:, None], (seq_group, length)).reshape(1, seq_group * length)
    send = head_stats(parts, (labels - me * width)[None, :], slots, head.T, seq_group, length)
    got = lax.all_to_all(send, "vocab", split_axis=0, concat_axis=0, tiled=True)
    return pl.pallas_call(combine_kernel, out_shape=jax.ShapeDtypeStruct((own_count, length), jnp.float32))(
        got.reshape(shards, own_count, 2 * length)
    )


def solution(mesh):
    return jax.shard_map(
        local,
        mesh=mesh,
        in_specs=(P(("dp", "vocab"), None), P("dp"), P("dp", None), P(None, "vocab")),
        out_specs=P(("dp", "vocab"), None),
        check_vma=False,
    )
```

time: 66.2 us -> 63.9 us (0.965)
  Pallas kernels: 40 us -> 38.6 us
  waiting for transfers between devices: 4.65 us -> 5.74 us
  other arithmetic: 1.92 us -> 1.25 us
    pallas_call x1 -> x2, Pallas kernels: 40 us -> 38.6 us  [the longest x1 37.2 us: head_stats(): pl.pallas_call(functools.partial(head_kernel, pieces=len(parts), chunk=ch...]
    ppermute x7, waiting for transfers between devices: 4.65 us -> 5.74 us  [swap(): return lax.ppermute(v, 'vocab', [(i, i ^ k) for i in range(shards)])]
    unnamed x11 -> x16, local copies, waits for them, and re-layouts: 2.37 us -> 1.45 us
    all_to_all x2, local copies, waits for them, and re-layouts: 0.52 us -> 1.23 us  [local(): got = lax.all_to_all(send, 'vocab', split_axis=0, concat_axis=0, tiled=True)]
  transfers between devices with their start and end apart: 7 -> 7, of which waited for: 3 -> 4; matrix products, arithmetic and copies ran while one was open for 6% -> 6% of each run, Pallas kernels for 0% -> 0%
where the time goes in v2:
time: 63.9 us; the launch traced here: 63.5 us
  Pallas kernels  38.6 us (60%)
  blocking collectives  7.29 us (11%)
  waiting for transfers between devices  5.74 us (9%)
  local copies, waits for them, and re-layouts  5.68 us (9%)
  starting transfers between devices  4.99 us (8%)
  other arithmetic  1.25 us (2%)
    pallas_call x1, Pallas kernels, head_stats(): pl.pallas_call(functools.partial(head_kernel, pieces=len(parts), chunk=ch...  37.2 us
    all_to_all x1, blocking collectives, local(): got = lax.all_to_all(send, 'vocab', split_axis=0, concat_axis=0, tiled=True)  7.29 us
    ppermute x7, waiting for transfers between devices, swap(): return lax.ppermute(v, 'vocab', [(i, i ^ k) for i in range(shards)])  5.74 us
    ppermute x7, starting transfers between devices, swap(): return lax.ppermute(v, 'vocab', [(i, i ^ k) for i in range(shards)])  4.99 us
    unnamed x16, local copies, waits for them, and re-layouts  1.45 us
    pallas_call x1, Pallas kernels, local(): pl.pallas_call(combine_kernel, out_shape=jax.ShapeDtypeStruct((own_count,...  1.37 us
  transfers between devices with their start and end apart: 7, of which 4 were waited for; matrix products, arithmetic and copies ran while one was open for 6% of the time, Pallas kernels for 0%

profile of v2, /device:TPU:0, one launch (start us, length us, event | category | flops | bytes accessed | tf_op | source)
XLA Modules:
  0.0 63.5 jit_solution(16274247202032398534)
XLA Ops:
  0.0 3.0 %collective-permute-start = (bf16[96,896]{1,0:T(8,128)(2,1)}, bf16[96,896]{1,0:T(8,128)(2,1)S(1)}, u32[]{:S(2)}, u32[]{:S(2)}) collective-permute-start(bf16[96,896]{1,0:T(8,128)(2,1)} %refs_0_.1), channel_id=1, source_target_pairs={{0,2},{1,3},{2,0},{3,1},{4,6},{5,7},{6,4},{7,5},{8,10},{9,11},{10,... | collective-permute-start | bytes 516104 | tf_op jit(solution)/shard_map/ppermute | solution.py:132
  3.0 1.5 %collective-permute-start.1 = (bf16[96,896]{1,0:T(8,128)(2,1)}, bf16[96,896]{1,0:T(8,128)(2,1)S(1)}, u32[]{:S(2)}, u32[]{:S(2)}) collective-permute-start(bf16[96,896]{1,0:T(8,128)(2,1)} %refs_0_.1), channel_id=1, source_target_pairs={{0,4},{1,5},{2,6},{3,7},{4,0},{5,1},{6,2},{7,3},{8,12},{9,13},{10,... | collective-permute-start | bytes 516104 | tf_op jit(solution)/shard_map/ppermute | solution.py:132
  4.5 0.0 collective-permute-start.3
  4.5 1.0 %fusion.7 = (s32[3]{0:T(128)S(1)}, s32[3]{0:T(128)S(1)}, s32[3]{0:T(128)S(1)}, s32[3]{0:T(128)S(1)}, s32[3]{0:T(128)S(1)}, /*index=5*/s32[3]{0:T(128)S(1)}, s32[3]{0:T(128)S(1)}, s32[3]{0:T(128)S(1)}) fusion(s32[1,24]{1,0:T(1,128)} %param.6, s32[]{:T(128)S(6)} %select_n.63, s32[]{:T(128)S(6)} %select_n.61, s32[]{:T(128)S(6)} %select_n.60, s32[]{:T(128)S(6)} %select_n.59, ...), kind=kLoop, calls=%fused_computation.16 | loop fusion | bytes 224 | tf_op jit(solution)/shard_map/dynamic_slice | solution.py:139
  5.5 0.1 concatenate.38
  5.6 0.1 broadcast_in_dim.2
  5.7 0.7 %reshape.123.refs_9_ = s32[1,768]{1,0:T(1,128)} reshape(s32[24,32]{1,0:T(8,128)S(1)} %broadcast_in_dim.2) | data formatting | bytes 6144 | tf_op jit(solution)/shard_map/reshape | solution.py:140
  6.3 1.1 %dynamic-slice_bitcast_fusion = (s32[1,96]{1,0:T(1,128)S(1)}, s32[1,96]{1,0:T(1,128)S(1)}, s32[1,96]{1,0:T(1,128)S(1)}, s32[1,96]{1,0:T(1,128)S(1)}, s32[1,96]{1...) fusion(s32[768]{0:T(1024)} %param.5, s32[]{:T(128)S(6)} %select_n.55, ...), kind=kLoop, calls=%fused_computation.17 | loop fusion | bytes 6176 | tf_op jit(solution)/shard_map/concatenate | solution.py:138
  7.4 0.1 concatenate.37
  7.5 0.9 %collective-permute-done.refs_1_ = bf16[96,896]{1,0:T(8,128)(2,1)S(1)} collective-permute-done((bf16[96,896]{1,0:T(8,128)(2,1)}, bf16[96,896]{1,0:T(8,128)(2,1)S(1)}, u32[]{:S(2)}, u32[]{:S(2)}) %collective-permute-start) | collective-permute-done | bytes 172064 | tf_op jit(solution)/shard_map/ppermute | solution.py:132
  8.4 0.0 collective-permute-start.4
  8.4 4.3 %collective-permute-done.1.refs_2_ = bf16[96,896]{1,0:T(8,128)(2,1)S(1)} collective-permute-done((bf16[96,896]{1,0:T(8,128)(2,1)}, bf16[96,896]{1,0:T(8,128)(2,1)S(1)}, u32[]{:S(2)}, u32[]{:S(2)}) %collective-permute-start.1) | collective-permute-done | bytes 172064 | tf_op jit(solution)/shard_map/ppermute | solution.py:132
  12.7 0.0 collective-permute-start.5
  12.7 0.0 collective-permute-done.2.refs_3_
  12.7 0.5 collective-permute-start.6
  13.2 0.6 broadcast_subtract_fusion.refs_8_
  13.8 0.0 collective-permute-done.3.refs_4_
  13.8 0.0 collective-permute-done.4.refs_5_
  13.8 0.3 collective-permute-done.5.refs_6_
  14.1 0.2 collective-permute-done.6.refs_7_
  14.4 0.1 copy-done.3
  14.5 0.1 copy-done.4
  14.5 0.2 copy-done.5
  14.8 0.3 copy-done.6
  15.0 37.2 %shard_map.46 = f32[24,64]{1,0:T(8,128)} custom-call(bf16[96,896]{1,0:T(8,128)(2,1)} %refs_0_.1, bf16[96,896]{1,0:T(8,128)(2,1)} %copy-done, bf16[96,896]{1,0:T(8,128)(2,1)} %copy-done.1, bf16[96,896]{1,0:T(8,128)(2,1)} %copy-done.2, bf16[96,896]{1,0:T(8,128)(2,1)} %copy-done.3, bf16[96,896]{1,0:T(8,128)(2,1)} %copy-done.4, bf16[96,896]{1,0:T(8,128)(2,1)} %copy-done.5, ...), custom_call_target="tpu_custom_call" | custom-call | tf_op jit(solution)/shard_map/pallas_call | solution.py:95
  52.2 0.7 %all_to_all.6 = f32[8,3,64]{2,1,0:T(4,128)S(1)} reshape(f32[24,64]{1,0:T(8,128)} %shard_map.46) | data formatting | bytes 12288 | tf_op jit(solution)/shard_map/all_to_all | solution.py:142
  52.9 0.1 reshape.124
  53.0 7.3 %all_to_all.9 = f32[8,1,192]{2,1,0:T(1,128)S(1)} all-to-all(f32[8,1,192]{2,1,0:T(1,128)S(1)} %reshape.124), channel_id=1, replica_groups=mesh['dp'=4,'vocab'=8] {'vocab'}, dimensions={0} | all-to-all | bytes 12288 | tf_op jit(solution)/shard_map/all_to_all | solution.py:142
  60.3 0.5 broadcast.8
  60.8 0.7 %reduce = f32[8,192]{1,0:T(8,128)S(1)} reduce(f32[8,1,192]{2,1,0:T(1,128)S(1)} %all_to_all.9, f32[]{:T(128)} %broadcast.8), dimensions={1}, to_apply=%all_to_all.7.reduce_sub_computation | reduce | bytes 12292 | tf_op jit(solution)/shard_map/all_to_all | solution.py:142
  61.5 0.7 %reshape.125.got_ref = f32[8,3,64]{2,1,0:T(4,128)} reshape(f32[8,192]{1,0:T(8,128)S(1)} %reduce) | data formatting | bytes 12288
  62.2 1.4 %shard_map.47 = f32[3,32]{1,0:T(4,128)} custom-call(f32[8,3,64]{2,1,0:T(4,128)} %reshape.125.got_ref), custom_call_target="tpu_custom_call" | custom-call | tf_op jit(solution)/shard_map/pallas_call | solution.py:143
  (11 shorter events, 0.0 us)
Async XLA Ops:
  0.0 8.4 %collective-permute-start = (bf16[96,896]{1,0:T(8,128)(2,1)}, bf16[96,896]{1,0:T(8,128)(2,1)S(1)}, u32[]{:S(2)}, u32[]{:S(2)}) collective-permute-start(bf16[96,896]{1,0:T(8,128)(2,1)} %refs_0_.1), channel_id=1, source_target_pairs={{0,2},{1,3},{2,0},{3,1},{4,6},{5,7},{6,4},{7,5},{8,10},{9,11},{10,... | collective-permute-start | bytes 516104 | tf_op jit(solution)/shard_map/ppermute | solution.py:132
  3.0 9.7 %collective-permute-start.1 = (bf16[96,896]{1,0:T(8,128)(2,1)}, bf16[96,896]{1,0:T(8,128)(2,1)S(1)}, u32[]{:S(2)}, u32[]{:S(2)}) collective-permute-start(bf16[96,896]{1,0:T(8,128)(2,1)} %refs_0_.1), channel_id=1, source_target_pairs={{0,4},{1,5},{2,6},{3,7},{4,0},{5,1},{6,2},{7,3},{8,12},{9,13},{10,... | collective-permute-start | bytes 516104 | tf_op jit(solution)/shard_map/ppermute | solution.py:132
  4.5 8.2 %collective-permute-start.2 = (bf16[96,896]{1,0:T(8,128)(2,1)}, bf16[96,896]{1,0:T(8,128)(2,1)S(1)}, u32[]{:S(2)}, u32[]{:S(2)}) collective-permute-start(bf16[96,896]{1,0:T(8,128)(2,1)} %refs_0_.1), channel_id=1, source_target_pairs={{0,6},{1,7},{2,4},{3,5},{4,2},{5,3},{6,0},{7,1},{8,14},{9,15},{10,... | collective-permute-start | bytes 516104 | tf_op jit(solution)/shard_map/ppermute | solution.py:132
  4.5 9.3 %collective-permute-start.3 = (bf16[96,896]{1,0:T(8,128)(2,1)}, bf16[96,896]{1,0:T(8,128)(2,1)S(1)}, u32[]{:S(2)}, u32[]{:S(2)}) collective-permute-start(bf16[96,896]{1,0:T(8,128)(2,1)} %refs_0_.1), channel_id=1, source_target_pairs={{0,1},{1,0},{2,3},{3,2},{4,5},{5,4},{6,7},{7,6},{8,9},{9,8},{10,11... | collective-permute-start | bytes 516104 | tf_op jit(solution)/shard_map/ppermute | solution.py:132
  8.4 6.0 %copy-start = (bf16[96,896]{1,0:T(8,128)(2,1)}, bf16[96,896]{1,0:T(8,128)(2,1)S(1)}, u32[]{:S(2)}) copy-start(bf16[96,896]{1,0:T(8,128)(2,1)S(1)} %collective-permute-done.refs_1_) | copy-start | bytes 516100
  8.4 5.4 %collective-permute-start.4 = (bf16[96,896]{1,0:T(8,128)(2,1)S(1)}, bf16[96,896]{1,0:T(8,128)(2,1)S(1)}, u32[]{:S(2)}, u32[]{:S(2)}) collective-permute-start(bf16[96,896]{1,0:T(8,128)(2,1)S(1)} %collective-permute-done.refs_1_), channel_id=1, source_target_pairs={{0,1},{1,0},{2,3},{3,2},{4,5},{5,4},{6,7},{7,6},{8,9},{9,8},{10,11... | collective-permute-start | bytes 516104 | tf_op jit(solution)/shard_map/ppermute | solution.py:132
  12.7 1.7 %copy-start.1 = (bf16[96,896]{1,0:T(8,128)(2,1)}, bf16[96,896]{1,0:T(8,128)(2,1)S(1)}, u32[]{:S(2)}) copy-start(bf16[96,896]{1,0:T(8,128)(2,1)S(1)} %collective-permute-done.1.refs_2_) | copy-start | bytes 516100
  12.7 1.4 %collective-permute-start.5 = (bf16[96,896]{1,0:T(8,128)(2,1)S(1)}, bf16[96,896]{1,0:T(8,128)(2,1)S(1)}, u32[]{:S(2)}, u32[]{:S(2)}) collective-permute-start(bf16[96,896]{1,0:T(8,128)(2,1)S(1)} %collective-permute-done.1.refs_2_), channel_id=1, source_target_pairs={{0,1},{1,0},{2,3},{3,2},{4,5},{5,4},{6,7},{7,6},{8,9},{9,8},{10,11... | collective-permute-start | bytes 516104 | tf_op jit(solution)/shard_map/ppermute | solution.py:132
  12.7 1.7 %copy-start.2 = (bf16[96,896]{1,0:T(8,128)(2,1)}, bf16[96,896]{1,0:T(8,128)(2,1)S(1)}, u32[]{:S(2)}) copy-start(bf16[96,896]{1,0:T(8,128)(2,1)S(1)} %collective-permute-done.2.refs_3_) | copy-start | bytes 516100
  12.7 1.6 %collective-permute-start.6 = (bf16[96,896]{1,0:T(8,128)(2,1)S(1)}, bf16[96,896]{1,0:T(8,128)(2,1)S(1)}, u32[]{:S(2)}, u32[]{:S(2)}) collective-permute-start(bf16[96,896]{1,0:T(8,128)(2,1)S(1)} %collective-permute-done.2.refs_3_), channel_id=1, source_target_pairs={{0,1},{1,0},{2,3},{3,2},{4,5},{5,4},{6,7},{7,6},{8,9},{9,8},{10,11... | collective-permute-start | bytes 516104 | tf_op jit(solution)/shard_map/ppermute | solution.py:132
  13.8 0.7 %copy-start.3 = (bf16[96,896]{1,0:T(8,128)(2,1)}, bf16[96,896]{1,0:T(8,128)(2,1)S(1)}, u32[]{:S(2)}) copy-start(bf16[96,896]{1,0:T(8,128)(2,1)S(1)} %collective-permute-done.3.refs_4_) | copy-start | bytes 516100
  13.8 0.7 %copy-start.4 = (bf16[96,896]{1,0:T(8,128)(2,1)}, bf16[96,896]{1,0:T(8,128)(2,1)S(1)}, u32[]{:S(2)}) copy-start(bf16[96,896]{1,0:T(8,128)(2,1)S(1)} %collective-permute-done.4.refs_5_) | copy-start | bytes 516100
  14.1 0.7 %copy-start.5 = (bf16[96,896]{1,0:T(8,128)(2,1)}, bf16[96,896]{1,0:T(8,128)(2,1)S(1)}, u32[]{:S(2)}) copy-start(bf16[96,896]{1,0:T(8,128)(2,1)S(1)} %collective-permute-done.5.refs_6_) | copy-start | bytes 516100
  14.4 0.7 %copy-start.6 = (bf16[96,896]{1,0:T(8,128)(2,1)}, bf16[96,896]{1,0:T(8,128)(2,1)S(1)}, u32[]{:S(2)}) copy-start(bf16[96,896]{1,0:T(8,128)(2,1)S(1)} %collective-permute-done.6.refs_7_) | copy-start | bytes 516100

commit v3 on v2

v3 whole, which is shorter than its diff:
```python
import functools
import math

import jax
import jax.numpy as jnp
from jax import lax
from jax.experimental import pallas as pl
from jax.experimental.pallas import tpu as pltpu
from jax.sharding import PartitionSpec as P

LOG2E = math.log2(math.e)
FLOOR = -1e30


def tree(op, values):
    while len(values) > 1:
        paired = [op(a, b) for a, b in zip(values[::2], values[1::2])]
        values = paired + ([values[-1]] if len(values) % 2 else [])
    return values[0]


def head_kernel(*refs, pieces, block, chunk, pull, width, group, length, shards):
    parts = refs[:pieces]
    lab_any, slot_any, w_any, o_ref = refs[pieces : pieces + 4]
    m_ref, s_ref, p_ref, lb_ref, lab_ref, slot_ref, x_ref, xt_ref, w_ref, sems, head_sems = refs[pieces + 4 :]
    tokens = x_ref.shape[0]
    blocks = w_ref.shape[0] // block

    copies, at = [], 0
    for part in parts:
        copies.append((part, x_ref.at[pl.ds(at, part.shape[0]), :]))
        at += part.shape[0]
    copies += [(lab_any, lab_ref), (slot_any, slot_ref)]
    copies = [pltpu.make_async_copy(src, dst, sems.at[i]) for i, (src, dst) in enumerate(copies)]

    def head_copy(index, count):
        rows = pl.ds(pl.multiple_of(index * pull, 8), count)
        return pltpu.make_async_copy(w_any.at[rows, :], w_ref.at[rows, :], head_sems.at[index])

    counts = [min(pull, width - start) for start in range(0, width, pull)]
    for copy in copies:
        copy.start()
    for index, count in enumerate(counts):
        head_copy(index, count).start()

    def labels():
        value = lab_ref[...]
        return jnp.where((value >= 0) & (value < width), value, -(1 << 30))

    m_ref[...] = jnp.full_like(m_ref, FLOOR)
    s_ref[...] = jnp.zeros_like(s_ref)
    p_ref[...] = jnp.zeros_like(p_ref)
    for copy in copies:
        copy.wait()
    lb_ref[...] = jnp.broadcast_to(jnp.right_shift(labels(), 3), lb_ref.shape)
    xt_ref[...] = x_ref[...].T

    sub = lax.broadcasted_iota(jnp.int32, (8, 128), 0)

    def run(step, masked):
        for r0 in range(0, block, chunk):
            if r0 % pull == 0:
                index = step * (block // pull) + r0 // pull
                if not masked:
                    head_copy(index, pull).wait()
                elif index < len(counts):
                    head_copy(index, counts[index]).wait()
            rows = pl.ds(pl.multiple_of(step * block + r0, 16), chunk)
            logits = jnp.dot(w_ref[rows, :], xt_ref[...], preferred_element_type=jnp.float32)
            for c in range(tokens // 128):
                cols = slice(c * 128, (c + 1) * 128)
                pick, top, total = p_ref[:, cols], m_ref[:, cols], s_ref[:, cols]
                label = lb_ref[:, cols] - (step * (block // 8) + r0 // 8)
                for g in range(0, chunk, group):
                    values = []
                    for r in range(g, min(g + group, chunk), 8):
                        value = logits[r : r + 8, cols]
                        if masked:
                            value = jnp.where(sub + (step * block + r0 + r) < width, value, FLOOR)
                        pick = jnp.where(label == r // 8, value, pick)
                        values.append(value)
                    peak = jnp.maximum(top, tree(jnp.maximum, values))
                    fresh = tree(jnp.add, [jnp.exp2((v - peak) * LOG2E) for v in values])
                    total = total * jnp.exp2((top - peak) * LOG2E) + fresh
                    top = peak
                p_ref[:, cols], m_ref[:, cols], s_ref[:, cols] = pick, top, total

    def body(step, carry):
        run(step, False)
        return carry

    lax.fori_loop(0, blocks - 1, body, 0)
    run(blocks - 1, True)

    top = m_ref[...]
    peak = jnp.max(top, axis=0, keepdims=True)
    total = jnp.sum(s_ref[...] * jnp.exp2((top - peak) * LOG2E), axis=0, keepdims=True)
    lse = peak + jnp.log(total)
    eight = lax.broadcasted_iota(jnp.int32, p_ref.shape, 0)
    picked = jnp.sum(jnp.where((labels() & 7) == eight, p_ref[...], 0.0), axis=0, keepdims=True)
    per_shard = o_ref.shape[2] // (2 * length)
    first = lax.broadcasted_iota(jnp.int32, (shards, tokens), 0) * per_shard
    token = lax.broadcasted_iota(jnp.int32, (tokens, length), 0)
    lane = lax.broadcasted_iota(jnp.int32, (tokens, length), 1)
    spread = (lax.rem(token, length) == lane).astype(jnp.float32)
    for i in range(per_shard):
        mine = first + i == slot_ref[...]
        for k, row in enumerate((lse, picked)):
            placed = jnp.dot(
                jnp.where(mine, row, 0.0), spread, precision=lax.Precision.HIGHEST, preferred_element_type=jnp.float32
            )
            lanes = slice((2 * i + k) * length, (2 * i + k + 1) * length)
            for d in range(shards):
                o_ref[d, :, lanes] = placed[d : d + 1, :]


def head_stats(parts, labels, slots, rows, shards, per_shard, length):
    tokens = labels.shape[1]
    width, depth = rows.shape
    block, chunk, pull = 3168, 144, 1584
    blocks = pl.cdiv(width, block)
    return pl.pallas_call(
        functools.partial(
            head_kernel,
            pieces=len(parts),
            block=block,
            chunk=chunk,
            pull=pull,
            width=width,
            group=24,
            length=length,
            shards=shards,
        ),
        out_shape=jax.ShapeDtypeStruct((shards, 1, 2 * length * per_shard), jnp.float32),
        in_specs=[pl.BlockSpec(memory_space=pl.ANY)] * (len(parts) + 3),
        out_specs=pl.BlockSpec(memory_space=pltpu.VMEM),
        scratch_shapes=[pltpu.VMEM((8, tokens), jnp.float32)] * 3
        + [
            pltpu.VMEM((8, tokens), jnp.int32),
            pltpu.VMEM((1, tokens), jnp.int32),
            pltpu.VMEM((1, tokens), jnp.int32),
            pltpu.VMEM((tokens, depth), parts[0].dtype),
            pltpu.VMEM((depth, tokens), parts[0].dtype),
            pltpu.VMEM((blocks * block, depth), rows.dtype),
            pltpu.SemaphoreType.DMA((len(parts) + 2,)),
            pltpu.SemaphoreType.DMA((pl.cdiv(width, pull),)),
        ],
        compiler_params=pltpu.CompilerParams(vmem_limit_bytes=46 << 20),
    )(*parts, labels, slots, rows)


def combine_kernel(got_ref, o_ref):
    count, length = o_ref.shape
    got = got_ref[:, 0, :]
    top = jnp.max(got, axis=0, keepdims=True)
    lse = top + jnp.log(jnp.sum(jnp.exp(got - top), axis=0, keepdims=True))
    picked = jnp.sum(got, axis=0, keepdims=True)
    for i in range(count):
        at = 2 * i * length
        o_ref[i : i + 1, :] = lse[:, at : at + length] - picked[:, at + length : at + 2 * length]


def local(hidden, target_ids, owner, head):
    shards, me = lax.axis_size("vocab"), lax.axis_index("vocab")
    width = head.shape[1]
    count = hidden.shape[0]
    seq_group = owner.shape[1]
    own_count = seq_group // shards
    length = target_ids.shape[0] // seq_group

    def swap(v, k):
        return lax.ppermute(v, "vocab", [(i, i ^ k) for i in range(shards)])

    places = list(range(0, shards, 2)) + list(range(1, shards, 2))
    even = [hidden] + [swap(hidden, k) for k in range(2, shards, 2)]
    parts = even + [swap(v, 1) for v in even]
    per_shard = count // length
    labels = jnp.concatenate([lax.dynamic_slice_in_dim(target_ids, (me ^ k) * count, count) for k in places])
    slots = jnp.concatenate([lax.dynamic_slice_in_dim(owner[0], (me ^ k) * per_shard, per_shard) for k in places])
    slots = jnp.broadcast_to(slots[:, None], (seq_group, length)).reshape(1, seq_group * length)
    labels = (labels - me * width)[None, :]
    send = head_stats(parts, labels, slots, head.T, shards, own_count, length)
    got = lax.all_to_all(send, "vocab", split_axis=0, concat_axis=0, tiled=True)
    return pl.pallas_call(combine_kernel, out_shape=jax.ShapeDtypeStruct((own_count, length), jnp.float32))(got)


def solution(mesh):
    return jax.shard_map(
        local,
        mesh=mesh,
        in_specs=(P(("dp", "vocab"), None), P("dp"), P("dp", None), P(None, "vocab")),
        out_specs=P(("dp", "vocab"), None),
        check_vma=False,
    )
```

time: 63.9 us -> 65.2 us (1.020)
  Pallas kernels: 38.6 us -> 42.4 us
  local copies, waits for them, and re-layouts: 5.68 us -> 3.34 us
  other arithmetic: 1.25 us -> 0.01 us
  waiting for transfers between devices: 5.74 us -> 6.72 us
    pallas_call x1, Pallas kernels: 37.2 us -> 41 us  [head_stats(): pl.pallas_call(functools.partial(head_kernel, pieces=len(parts), block=bl...]
    all_to_all x2 -> x0, local copies, waits for them, and re-layouts: 1.23 us -> none  [local(): got = lax.all_to_all(send, 'vocab', split_axis=0, concat_axis=0, tiled=True)]
    ppermute x7, waiting for transfers between devices: 5.74 us -> 6.72 us  [swap(): return lax.ppermute(v, 'vocab', [(i, i ^ k) for i in range(shards)])]
    all_to_all x1 -> x0, other arithmetic: 0.67 us -> none  [local(): got = lax.all_to_all(send, 'vocab', split_axis=0, concat_axis=0, tiled=True)]
    unnamed x16 -> x2, local copies, waits for them, and re-layouts: 1.45 us -> 0.92 us
  transfers between devices with their start and end apart: 7 -> 7, of which waited for: 4 -> 5; matrix products, arithmetic and copies ran while one was open for 6% -> 4% of each run, Pallas kernels for 0% -> 0%
where the time goes in v3:
time: 65.2 us; the launch traced here: 65 us
  Pallas kernels  42.4 us (65%)
  blocking collectives  7.74 us (12%)
  waiting for transfers between devices  6.72 us (10%)
  starting transfers between devices  4.73 us (7%)
  local copies, waits for them, and re-layouts  3.34 us (5%)
    pallas_call x1, Pallas kernels, head_stats(): pl.pallas_call(functools.partial(head_kernel, pieces=len(parts), block=bl...  41 us
    all_to_all x1, blocking collectives, local(): got = lax.all_to_all(send, 'vocab', split_axis=0, concat_axis=0, tiled=True)  7.74 us
    ppermute x7, waiting for transfers between devices, swap(): return lax.ppermute(v, 'vocab', [(i, i ^ k) for i in range(shards)])  6.72 us
    ppermute x7, starting transfers between devices, swap(): return lax.ppermute(v, 'vocab', [(i, i ^ k) for i in range(shards)])  4.73 us
    pallas_call x1, Pallas kernels, local(): pl.pallas_call(combine_kernel, out_shape=jax.ShapeDtypeStruct((own_count,...  1.42 us
  transfers between devices with their start and end apart: 7, of which 5 were waited for; matrix products, arithmetic and copies ran while one was open for 4% of the time, Pallas kernels for 0%

profile of v3, /device:TPU:0, one launch (start us, length us, event | category | flops | bytes accessed | tf_op | source)
XLA Modules:
  0.0 65.0 jit_solution(3360926232892520625)
XLA Ops:
  0.0 3.9 %collective-permute-start.2 = (bf16[96,896]{1,0:T(8,128)(2,1)}, bf16[96,896]{1,0:T(8,128)(2,1)S(1)}, u32[]{:S(2)}, u32[]{:S(2)}) collective-permute-start(bf16[96,896]{1,0:T(8,128)(2,1)} %refs_0_.1), channel_id=1, source_target_pairs={{0,6},{1,7},{2,4},{3,5},{4,2},{5,3},{6,0},{7,1},{8,14},{9,15},{10,... | collective-permute-start | bytes 516104 | tf_op jit(solution)/shard_map/ppermute | solution.py:172
  3.9 0.5 collective-permute-start.1
  4.4 0.1 collective-permute-start
  4.5 0.0 collective-permute-start.3
  4.5 1.0 %fusion.7 = (s32[3]{0:T(128)S(1)}, s32[3]{0:T(128)S(1)}, s32[3]{0:T(128)S(1)}, s32[3]{0:T(128)S(1)}, s32[3]{0:T(128)S(1)}, /*index=5*/s32[3]{0:T(128)S(1)}, s32[3]{0:T(128)S(1)}, s32[3]{0:T(128)S(1)}) fusion(s32[1,24]{1,0:T(1,128)} %param.6, s32[]{:T(128)S(6)} %select_n.63, s32[]{:T(128)S(6)} %select_n.61, s32[]{:T(128)S(6)} %select_n.60, s32[]{:T(128)S(6)} %select_n.59, ...), kind=kLoop, calls=%fused_computation.16 | loop fusion | bytes 224 | tf_op jit(solution)/shard_map/dynamic_slice | solution.py:179
  5.5 0.1 concatenate.38
  5.6 0.1 broadcast_in_dim.2
  5.7 0.1 reshape.119.refs_9_
  5.8 1.1 %dynamic-slice_bitcast_fusion = (s32[1,96]{1,0:T(1,128)S(1)}, s32[1,96]{1,0:T(1,128)S(1)}, s32[1,96]{1,0:T(1,128)S(1)}, s32[1,96]{1,0:T(1,128)S(1)}, s32[1,96]{1...) fusion(s32[768]{0:T(1024)} %param.5, s32[]{:T(128)S(6)} %select_n.55, ...), kind=kLoop, calls=%fused_computation.17 | loop fusion | bytes 6176 | tf_op jit(solution)/shard_map/concatenate | solution.py:178
  6.8 0.1 concatenate.37
  6.9 2.4 %collective-permute-done.2.refs_3_ = bf16[96,896]{1,0:T(8,128)(2,1)S(1)} collective-permute-done((bf16[96,896]{1,0:T(8,128)(2,1)}, bf16[96,896]{1,0:T(8,128)(2,1)S(1)}, u32[]{:S(2)}, u32[]{:S(2)}) %collective-permute-start.2) | collective-permute-done | bytes 172064 | tf_op jit(solution)/shard_map/ppermute | solution.py:172
  9.4 0.0 collective-permute-start.6
  9.4 2.8 %collective-permute-done.1.refs_2_ = bf16[96,896]{1,0:T(8,128)(2,1)S(1)} collective-permute-done((bf16[96,896]{1,0:T(8,128)(2,1)}, bf16[96,896]{1,0:T(8,128)(2,1)S(1)}, u32[]{:S(2)}, u32[]{:S(2)}) %collective-permute-start.1) | collective-permute-done | bytes 172064 | tf_op jit(solution)/shard_map/ppermute | solution.py:172
  12.2 0.0 collective-permute-start.5
  12.2 0.3 collective-permute-done.refs_1_
  12.5 0.2 collective-permute-start.4
  12.7 0.0 collective-permute-done.3.refs_4_
  12.7 0.0 collective-permute-done.6.refs_7_
  12.7 0.9 %collective-permute-done.5.refs_6_ = bf16[96,896]{1,0:T(8,128)(2,1)S(1)} collective-permute-done((bf16[96,896]{1,0:T(8,128)(2,1)S(1)}, bf16[96,896]{1,0:T(8,128)(2,1)S(1)}, u32[]{:S(2)}, u32[]{:S(2)}) %collective-permute-start.5) | collective-permute-done | bytes 172064 | tf_op jit(solution)/shard_map/ppermute | solution.py:172
  13.6 0.3 collective-permute-done.4.refs_5_
  13.9 0.0 copy-start
  13.9 0.9 %copy-done = bf16[96,896]{1,0:T(8,128)(2,1)S(1)} copy-done((bf16[96,896]{1,0:T(8,128)(2,1)S(1)}, bf16[96,896]{1,0:T(8,128)(2,1)}, u32[]{:S(2)}) %copy-start) | copy-done | bytes 172056
  14.8 41.0 %shard_map.46 = f32[8,1,192]{2,1,0:T(1,128)S(1)} custom-call(bf16[96,896]{1,0:T(8,128)(2,1)S(1)} %copy-done, bf16[96,896]{1,0:T(8,128)(2,1)S(1)} %collective-permute-done.refs_1_, bf16[96,896]{1,0:T(8,128)(2,1)S(1)} %collective-permute-done.1.refs_2_, bf16[96,896]{1,0:T(8,128)(2,1)S(1)} %collective-permute-done.2.refs_3_, ...), custom_call_target="tpu_custom_call" | custom-call | tf_op jit(solution)/shard_map/pallas_call | solution.py:122
  55.8 7.7 %all_to_all.5.got_ref = f32[8,1,192]{2,1,0:T(1,128)} all-to-all(f32[8,1,192]{2,1,0:T(1,128)S(1)} %shard_map.46), channel_id=1, replica_groups=mesh['dp'=4,'vocab'=8] {'vocab'}, dimensions={0} | all-to-all | bytes 12288 | tf_op jit(solution)/shard_map/all_to_all | solution.py:183
  63.5 1.4 %shard_map.47 = f32[3,32]{1,0:T(4,128)} custom-call(f32[8,1,192]{2,1,0:T(1,128)} %all_to_all.5.got_ref), custom_call_target="tpu_custom_call" | custom-call | tf_op jit(solution)/shard_map/pallas_call | solution.py:184
  (1 shorter events, 0.0 us)
Async XLA Ops:
  0.0 9.4 %collective-permute-start.2 = (bf16[96,896]{1,0:T(8,128)(2,1)}, bf16[96,896]{1,0:T(8,128)(2,1)S(1)}, u32[]{:S(2)}, u32[]{:S(2)}) collective-permute-start(bf16[96,896]{1,0:T(8,128)(2,1)} %refs_0_.1), channel_id=1, source_target_pairs={{0,6},{1,7},{2,4},{3,5},{4,2},{5,3},{6,0},{7,1},{8,14},{9,15},{10,... | collective-permute-start | bytes 516104 | tf_op jit(solution)/shard_map/ppermute | solution.py:172
  3.9 8.3 %collective-permute-start.1 = (bf16[96,896]{1,0:T(8,128)(2,1)}, bf16[96,896]{1,0:T(8,128)(2,1)S(1)}, u32[]{:S(2)}, u32[]{:S(2)}) collective-permute-start(bf16[96,896]{1,0:T(8,128)(2,1)} %refs_0_.1), channel_id=1, source_target_pairs={{0,4},{1,5},{2,6},{3,7},{4,0},{5,1},{6,2},{7,3},{8,12},{9,13},{10,... | collective-permute-start | bytes 516104 | tf_op jit(solution)/shard_map/ppermute | solution.py:172
  4.4 8.1 %collective-permute-start = (bf16[96,896]{1,0:T(8,128)(2,1)}, bf16[96,896]{1,0:T(8,128)(2,1)S(1)}, u32[]{:S(2)}, u32[]{:S(2)}) collective-permute-start(bf16[96,896]{1,0:T(8,128)(2,1)} %refs_0_.1), channel_id=1, source_target_pairs={{0,2},{1,3},{2,0},{3,1},{4,6},{5,7},{6,4},{7,5},{8,10},{9,11},{10,... | collective-permute-start | bytes 516104 | tf_op jit(solution)/shard_map/ppermute | solution.py:172
  4.5 8.2 %collective-permute-start.3 = (bf16[96,896]{1,0:T(8,128)(2,1)}, bf16[96,896]{1,0:T(8,128)(2,1)S(1)}, u32[]{:S(2)}, u32[]{:S(2)}) collective-permute-start(bf16[96,896]{1,0:T(8,128)(2,1)} %refs_0_.1), channel_id=1, source_target_pairs={{0,1},{1,0},{2,3},{3,2},{4,5},{5,4},{6,7},{7,6},{8,9},{9,8},{10,11... | collective-permute-start | bytes 516104 | tf_op jit(solution)/shard_map/ppermute | solution.py:172
  9.4 3.4 %collective-permute-start.6 = (bf16[96,896]{1,0:T(8,128)(2,1)S(1)}, bf16[96,896]{1,0:T(8,128)(2,1)S(1)}, u32[]{:S(2)}, u32[]{:S(2)}) collective-permute-start(bf16[96,896]{1,0:T(8,128)(2,1)S(1)} %collective-permute-done.2.refs_3_), channel_id=1, source_target_pairs={{0,1},{1,0},{2,3},{3,2},{4,5},{5,4},{6,7},{7,6},{8,9},{9,8},{10,11... | collective-permute-start | bytes 516104 | tf_op jit(solution)/shard_map/ppermute | solution.py:172
  12.2 1.4 %collective-permute-start.5 = (bf16[96,896]{1,0:T(8,128)(2,1)S(1)}, bf16[96,896]{1,0:T(8,128)(2,1)S(1)}, u32[]{:S(2)}, u32[]{:S(2)}) collective-permute-start(bf16[96,896]{1,0:T(8,128)(2,1)S(1)} %collective-permute-done.1.refs_2_), channel_id=1, source_target_pairs={{0,1},{1,0},{2,3},{3,2},{4,5},{5,4},{6,7},{7,6},{8,9},{9,8},{10,11... | collective-permute-start | bytes 516104 | tf_op jit(solution)/shard_map/ppermute | solution.py:172
  12.5 1.4 %collective-permute-start.4 = (bf16[96,896]{1,0:T(8,128)(2,1)S(1)}, bf16[96,896]{1,0:T(8,128)(2,1)S(1)}, u32[]{:S(2)}, u32[]{:S(2)}) collective-permute-start(bf16[96,896]{1,0:T(8,128)(2,1)S(1)} %collective-permute-done.refs_1_), channel_id=1, source_target_pairs={{0,1},{1,0},{2,3},{3,2},{4,5},{5,4},{6,7},{7,6},{8,9},{9,8},{10,11... | collective-permute-start | bytes 516104 | tf_op jit(solution)/shard_map/ppermute | solution.py:172
  13.9 0.9 %copy-start = (bf16[96,896]{1,0:T(8,128)(2,1)S(1)}, bf16[96,896]{1,0:T(8,128)(2,1)}, u32[]{:S(2)}) copy-start(bf16[96,896]{1,0:T(8,128)(2,1)} %refs_0_.1) | copy-start | bytes 516100

commit v4 on v2

--- a/solution.py
+++ b/solution.py
@@ -19,7 +19,7 @@
     return values[0]
 
 
-def head_kernel(*refs, pieces, chunk, width, group, length):
+def head_kernel(*refs, pieces, chunk, width, group, length, shards):
     parts, (lab_ref, slot_ref, w_ref, o_ref, m_ref, s_ref, p_ref, lb_ref, x_ref, xt_ref) = refs[:pieces], refs[pieces:]
     tokens = x_ref.shape[0]
     block = w_ref.shape[0]
@@ -77,24 +77,29 @@
         lse = peak + jnp.log(total)
         eight = lax.broadcasted_iota(jnp.int32, p_ref.shape, 0)
         picked = jnp.sum(jnp.where((labels() & 7) == eight, p_ref[...], 0.0), axis=0, keepdims=True)
-        slots = o_ref.shape[0]
-        mine = lax.broadcasted_iota(jnp.int32, (slots, tokens), 0) == slot_ref[...]
+        per_shard = o_ref.shape[2] // (2 * length)
+        first = lax.broadcasted_iota(jnp.int32, (shards, tokens), 0) * per_shard
         token = lax.broadcasted_iota(jnp.int32, (tokens, length), 0)
         lane = lax.broadcasted_iota(jnp.int32, (tokens, length), 1)
         spread = (lax.rem(token, length) == lane).astype(jnp.float32)
-        for k, row in enumerate((lse, picked)):
-            o_ref[:, k * length : (k + 1) * length] = jnp.dot(
-                jnp.where(mine, row, 0.0), spread, precision=lax.Precision.HIGHEST, preferred_element_type=jnp.float32
-            )
+        for i in range(per_shard):
+            mine = first + i == slot_ref[...]
+            for k, row in enumerate((lse, picked)):
+                placed = jnp.dot(
+                    jnp.where(mine, row, 0.0), spread, precision=lax.Precision.HIGHEST, preferred_element_type=jnp.float32
+                )
+                lanes = slice((2 * i + k) * length, (2 * i + k + 1) * length)
+                for d in range(shards):
+                    o_ref[d, :, lanes] = placed[d : d + 1, :]
 
 
-def head_stats(parts, labels, slots, rows, slot_count, length):
+def head_stats(parts, labels, slots, rows, shards, per_shard, length):
     tokens, depth = labels.shape[1], rows.shape[1]
     width = rows.shape[0]
     block, chunk = 3168, 144
     return pl.pallas_call(
-        functools.partial(head_kernel, pieces=len(parts), chunk=chunk, width=width, group=24, length=length),
-        out_shape=jax.ShapeDtypeStruct((slot_count, 2 * length), jnp.float32),
+        functools.partial(head_kernel, pieces=len(parts), chunk=chunk, width=width, group=24, length=length, shards=shards),
+        out_shape=jax.ShapeDtypeStruct((shards, 1, 2 * length * per_shard), jnp.float32),
         grid=(pl.cdiv(width, block),),
         in_specs=[pl.BlockSpec(part.shape, lambda j: (0, 0)) for part in parts]
         + [
@@ -102,22 +107,26 @@
             pl.BlockSpec((1, tokens), lambda j: (0, 0)),
             pl.BlockSpec((block, depth), lambda j: (j, 0)),
         ],
-        out_specs=pl.BlockSpec((slot_count, 2 * length), lambda j: (0, 0)),
+        out_specs=pl.BlockSpec((shards, 1, 2 * length * per_shard), lambda j: (0, 0, 0)),
         scratch_shapes=[pltpu.VMEM((8, tokens), jnp.float32)] * 3
         + [
             pltpu.VMEM((8, tokens), jnp.int32),
             pltpu.VMEM((tokens, depth), parts[0].dtype),
             pltpu.VMEM((depth, tokens), parts[0].dtype),
         ],
-        compiler_params=pltpu.CompilerParams(vmem_limit_bytes=60 << 20),
+        compiler_params=pltpu.CompilerParams(vmem_limit_bytes=40 << 20),
     )(*parts, labels, slots, rows)
 
 
 def combine_kernel(got_ref, o_ref):
-    length = o_ref.shape[1]
-    parts, picked = got_ref[:, :, :length], got_ref[:, :, length:]
-    top = jnp.max(parts, axis=0)
-    o_ref[...] = top + jnp.log(jnp.sum(jnp.exp(parts - top[None]), axis=0)) - jnp.sum(picked, axis=0)
+    count, length = o_ref.shape
+    got = got_ref[:, 0, :]
+    top = jnp.max(got, axis=0, keepdims=True)
+    lse = top + jnp.log(jnp.sum(jnp.exp(got - top), axis=0, keepdims=True))
+    picked = jnp.sum(got, axis=0, keepdims=True)
+    for i in range(count):
+        at = 2 * i * length
+        o_ref[i : i + 1, :] = lse[:, at : at + length] - picked[:, at + length : at + 2 * length]
 
 
 def local(hidden, target_ids, owner, head):
@@ -138,11 +147,10 @@
     labels = jnp.concatenate([lax.dynamic_slice_in_dim(target_ids, (me ^ k) * count, count) for k in places])
     slots = jnp.concatenate([lax.dynamic_slice_in_dim(owner[0], (me ^ k) * per_shard, per_shard) for k in places])
     slots = jnp.broadcast_to(slots[:, None], (seq_group, length)).reshape(1, seq_group * length)
-    send = head_stats(parts, (labels - me * width)[None, :], slots, head.T, seq_group, length)
+    labels = (labels - me * width)[None, :]
+    send = head_stats(parts, labels, slots, head.T, shards, own_count, length)
     got = lax.all_to_all(send, "vocab", split_axis=0, concat_axis=0, tiled=True)
-    return pl.pallas_call(combine_kernel, out_shape=jax.ShapeDtypeStruct((own_count, length), jnp.float32))(
-        got.reshape(shards, own_count, 2 * length)
-    )
+    return pl.pallas_call(combine_kernel, out_shape=jax.ShapeDtypeStruct((own_count, length), jnp.float32))(got)
 
 
 def solution(mesh):

time: 63.9 us -> 61 us (0.955)
  local copies, waits for them, and re-layouts: 5.68 us -> 3.34 us
  other arithmetic: 1.25 us -> 0.01 us
  waiting for transfers between devices: 5.74 us -> 6.72 us
    all_to_all x2 -> x0, local copies, waits for them, and re-layouts: 1.23 us -> none  [local(): got = lax.all_to_all(send, 'vocab', split_axis=0, concat_axis=0, tiled=True)]
    ppermute x7, waiting for transfers between devices: 5.74 us -> 6.72 us  [swap(): return lax.ppermute(v, 'vocab', [(i, i ^ k) for i in range(shards)])]
    all_to_all x1 -> x0, other arithmetic: 0.67 us -> none  [local(): got = lax.all_to_all(send, 'vocab', split_axis=0, concat_axis=0, tiled=True)]
    unnamed x16 -> x2, local copies, waits for them, and re-layouts: 1.45 us -> 0.92 us
  transfers between devices with their start and end apart: 7 -> 7, of which waited for: 4 -> 5; matrix products, arithmetic and copies ran while one was open for 6% -> 4% of each run, Pallas kernels for 0% -> 0%
where the time goes in v4:
time: 61 us; the launch traced here: 60.7 us
  Pallas kernels  38.1 us (62%)
  blocking collectives  7.74 us (13%)
  waiting for transfers between devices  6.72 us (11%)
  starting transfers between devices  4.73 us (8%)
  local copies, waits for them, and re-layouts  3.34 us (5%)
    pallas_call x1, Pallas kernels, head_stats(): pl.pallas_call(functools.partial(head_kernel, pieces=len(parts), chunk=ch...  36.7 us
    all_to_all x1, blocking collectives, local(): got = lax.all_to_all(send, 'vocab', split_axis=0, concat_axis=0, tiled=True)  7.74 us
    ppermute x7, waiting for transfers between devices, swap(): return lax.ppermute(v, 'vocab', [(i, i ^ k) for i in range(shards)])  6.72 us
    ppermute x7, starting transfers between devices, swap(): return lax.ppermute(v, 'vocab', [(i, i ^ k) for i in range(shards)])  4.73 us
    pallas_call x1, Pallas kernels, local(): pl.pallas_call(combine_kernel, out_shape=jax.ShapeDtypeStruct((own_count,...  1.42 us
  transfers between devices with their start and end apart: 7, of which 5 were waited for; matrix products, arithmetic and copies ran while one was open for 4% of the time, Pallas kernels for 0%

profile of v4, /device:TPU:0, one launch (start us, length us, event | category | flops | bytes accessed | tf_op | source)
XLA Modules:
  0.0 60.7 jit_solution(6131066493136011215)
XLA Ops:
  0.0 3.9 %collective-permute-start.2 = (bf16[96,896]{1,0:T(8,128)(2,1)}, bf16[96,896]{1,0:T(8,128)(2,1)S(1)}, u32[]{:S(2)}, u32[]{:S(2)}) collective-permute-start(bf16[96,896]{1,0:T(8,128)(2,1)} %refs_0_.1), channel_id=1, source_target_pairs={{0,6},{1,7},{2,4},{3,5},{4,2},{5,3},{6,0},{7,1},{8,14},{9,15},{10,... | collective-permute-start | bytes 516104 | tf_op jit(solution)/shard_map/ppermute | solution.py:141
  3.9 0.5 collective-permute-start.1
  4.4 0.1 collective-permute-start
  4.5 0.0 collective-permute-start.3
  4.5 1.0 %fusion.7 = (s32[3]{0:T(128)S(1)}, s32[3]{0:T(128)S(1)}, s32[3]{0:T(128)S(1)}, s32[3]{0:T(128)S(1)}, s32[3]{0:T(128)S(1)}, /*index=5*/s32[3]{0:T(128)S(1)}, s32[3]{0:T(128)S(1)}, s32[3]{0:T(128)S(1)}) fusion(s32[1,24]{1,0:T(1,128)} %param.6, s32[]{:T(128)S(6)} %select_n.63, s32[]{:T(128)S(6)} %select_n.61, s32[]{:T(128)S(6)} %select_n.60, s32[]{:T(128)S(6)} %select_n.59, ...), kind=kLoop, calls=%fused_computation.16 | loop fusion | bytes 224 | tf_op jit(solution)/shard_map/dynamic_slice | solution.py:148
  5.5 0.1 concatenate.38
  5.6 0.1 broadcast_in_dim.2
  5.7 0.1 reshape.119.refs_9_
  5.8 1.1 %dynamic-slice_bitcast_fusion = (s32[1,96]{1,0:T(1,128)S(1)}, s32[1,96]{1,0:T(1,128)S(1)}, s32[1,96]{1,0:T(1,128)S(1)}, s32[1,96]{1,0:T(1,128)S(1)}, s32[1,96]{1...) fusion(s32[768]{0:T(1024)} %param.5, s32[]{:T(128)S(6)} %select_n.55, ...), kind=kLoop, calls=%fused_computation.17 | loop fusion | bytes 6176 | tf_op jit(solution)/shard_map/concatenate | solution.py:147
  6.8 0.1 concatenate.37
  6.9 2.4 %collective-permute-done.2.refs_3_ = bf16[96,896]{1,0:T(8,128)(2,1)S(1)} collective-permute-done((bf16[96,896]{1,0:T(8,128)(2,1)}, bf16[96,896]{1,0:T(8,128)(2,1)S(1)}, u32[]{:S(2)}, u32[]{:S(2)}) %collective-permute-start.2) | collective-permute-done | bytes 172064 | tf_op jit(solution)/shard_map/ppermute | solution.py:141
  9.4 0.0 collective-permute-start.6
  9.4 2.8 %collective-permute-done.1.refs_2_ = bf16[96,896]{1,0:T(8,128)(2,1)S(1)} collective-permute-done((bf16[96,896]{1,0:T(8,128)(2,1)}, bf16[96,896]{1,0:T(8,128)(2,1)S(1)}, u32[]{:S(2)}, u32[]{:S(2)}) %collective-permute-start.1) | collective-permute-done | bytes 172064 | tf_op jit(solution)/shard_map/ppermute | solution.py:141
  12.2 0.0 collective-permute-start.5
  12.2 0.3 collective-permute-done.refs_1_
  12.5 0.2 collective-permute-start.4
  12.7 0.0 collective-permute-done.3.refs_4_
  12.7 0.0 collective-permute-done.6.refs_7_
  12.7 0.9 %collective-permute-done.5.refs_6_ = bf16[96,896]{1,0:T(8,128)(2,1)S(1)} collective-permute-done((bf16[96,896]{1,0:T(8,128)(2,1)S(1)}, bf16[96,896]{1,0:T(8,128)(2,1)S(1)}, u32[]{:S(2)}, u32[]{:S(2)}) %collective-permute-start.5) | collective-permute-done | bytes 172064 | tf_op jit(solution)/shard_map/ppermute | solution.py:141
  13.6 0.3 collective-permute-done.4.refs_5_
  13.9 0.0 copy-start
  13.9 0.9 %copy-done = bf16[96,896]{1,0:T(8,128)(2,1)S(1)} copy-done((bf16[96,896]{1,0:T(8,128)(2,1)S(1)}, bf16[96,896]{1,0:T(8,128)(2,1)}, u32[]{:S(2)}) %copy-start) | copy-done | bytes 172056
  14.8 36.7 %shard_map.46 = f32[8,1,192]{2,1,0:T(1,128)S(1)} custom-call(bf16[96,896]{1,0:T(8,128)(2,1)S(1)} %copy-done, bf16[96,896]{1,0:T(8,128)(2,1)S(1)} %collective-permute-done.refs_1_, bf16[96,896]{1,0:T(8,128)(2,1)S(1)} %collective-permute-done.1.refs_2_, bf16[96,896]{1,0:T(8,128)(2,1)S(1)} %collective-permute-done.2.refs_3_, ...), custom_call_target="tpu_custom_call" | custom-call | tf_op jit(solution)/shard_map/pallas_call | solution.py:100
  51.5 7.7 %all_to_all.5.got_ref = f32[8,1,192]{2,1,0:T(1,128)} all-to-all(f32[8,1,192]{2,1,0:T(1,128)S(1)} %shard_map.46), channel_id=1, replica_groups=mesh['dp'=4,'vocab'=8] {'vocab'}, dimensions={0} | all-to-all | bytes 12288 | tf_op jit(solution)/shard_map/all_to_all | solution.py:152
  59.3 1.4 %shard_map.47 = f32[3,32]{1,0:T(4,128)} custom-call(f32[8,1,192]{2,1,0:T(1,128)} %all_to_all.5.got_ref), custom_call_target="tpu_custom_call" | custom-call | tf_op jit(solution)/shard_map/pallas_call | solution.py:153
  (1 shorter events, 0.0 us)
Async XLA Ops:
  0.0 9.4 %collective-permute-start.2 = (bf16[96,896]{1,0:T(8,128)(2,1)}, bf16[96,896]{1,0:T(8,128)(2,1)S(1)}, u32[]{:S(2)}, u32[]{:S(2)}) collective-permute-start(bf16[96,896]{1,0:T(8,128)(2,1)} %refs_0_.1), channel_id=1, source_target_pairs={{0,6},{1,7},{2,4},{3,5},{4,2},{5,3},{6,0},{7,1},{8,14},{9,15},{10,... | collective-permute-start | bytes 516104 | tf_op jit(solution)/shard_map/ppermute | solution.py:141
  3.9 8.3 %collective-permute-start.1 = (bf16[96,896]{1,0:T(8,128)(2,1)}, bf16[96,896]{1,0:T(8,128)(2,1)S(1)}, u32[]{:S(2)}, u32[]{:S(2)}) collective-permute-start(bf16[96,896]{1,0:T(8,128)(2,1)} %refs_0_.1), channel_id=1, source_target_pairs={{0,4},{1,5},{2,6},{3,7},{4,0},{5,1},{6,2},{7,3},{8,12},{9,13},{10,... | collective-permute-start | bytes 516104 | tf_op jit(solution)/shard_map/ppermute | solution.py:141
  4.4 8.1 %collective-permute-start = (bf16[96,896]{1,0:T(8,128)(2,1)}, bf16[96,896]{1,0:T(8,128)(2,1)S(1)}, u32[]{:S(2)}, u32[]{:S(2)}) collective-permute-start(bf16[96,896]{1,0:T(8,128)(2,1)} %refs_0_.1), channel_id=1, source_target_pairs={{0,2},{1,3},{2,0},{3,1},{4,6},{5,7},{6,4},{7,5},{8,10},{9,11},{10,... | collective-permute-start | bytes 516104 | tf_op jit(solution)/shard_map/ppermute | solution.py:141
  4.5 8.2 %collective-permute-start.3 = (bf16[96,896]{1,0:T(8,128)(2,1)}, bf16[96,896]{1,0:T(8,128)(2,1)S(1)}, u32[]{:S(2)}, u32[]{:S(2)}) collective-permute-start(bf16[96,896]{1,0:T(8,128)(2,1)} %refs_0_.1), channel_id=1, source_target_pairs={{0,1},{1,0},{2,3},{3,2},{4,5},{5,4},{6,7},{7,6},{8,9},{9,8},{10,11... | collective-permute-start | bytes 516104 | tf_op jit(solution)/shard_map/ppermute | solution.py:141
  9.4 3.4 %collective-permute-start.6 = (bf16[96,896]{1,0:T(8,128)(2,1)S(1)}, bf16[96,896]{1,0:T(8,128)(2,1)S(1)}, u32[]{:S(2)}, u32[]{:S(2)}) collective-permute-start(bf16[96,896]{1,0:T(8,128)(2,1)S(1)} %collective-permute-done.2.refs_3_), channel_id=1, source_target_pairs={{0,1},{1,0},{2,3},{3,2},{4,5},{5,4},{6,7},{7,6},{8,9},{9,8},{10,11... | collective-permute-start | bytes 516104 | tf_op jit(solution)/shard_map/ppermute | solution.py:141
  12.2 1.4 %collective-permute-start.5 = (bf16[96,896]{1,0:T(8,128)(2,1)S(1)}, bf16[96,896]{1,0:T(8,128)(2,1)S(1)}, u32[]{:S(2)}, u32[]{:S(2)}) collective-permute-start(bf16[96,896]{1,0:T(8,128)(2,1)S(1)} %collective-permute-done.1.refs_2_), channel_id=1, source_target_pairs={{0,1},{1,0},{2,3},{3,2},{4,5},{5,4},{6,7},{7,6},{8,9},{9,8},{10,11... | collective-permute-start | bytes 516104 | tf_op jit(solution)/shard_map/ppermute | solution.py:141
  12.5 1.4 %collective-permute-start.4 = (bf16[96,896]{1,0:T(8,128)(2,1)S(1)}, bf16[96,896]{1,0:T(8,128)(2,1)S(1)}, u32[]{:S(2)}, u32[]{:S(2)}) collective-permute-start(bf16[96,896]{1,0:T(8,128)(2,1)S(1)} %collective-permute-done.refs_1_), channel_id=1, source_target_pairs={{0,1},{1,0},{2,3},{3,2},{4,5},{5,4},{6,7},{7,6},{8,9},{9,8},{10,11... | collective-permute-start | bytes 516104 | tf_op jit(solution)/shard_map/ppermute | solution.py:141
  13.9 0.9 %copy-start = (bf16[96,896]{1,0:T(8,128)(2,1)S(1)}, bf16[96,896]{1,0:T(8,128)(2,1)}, u32[]{:S(2)}) copy-start(bf16[96,896]{1,0:T(8,128)(2,1)} %refs_0_.1) | copy-start | bytes 516100
